TPU v7x, 128 devices: a whole 4x4x4 slice. The times are simulated.
128 devices in a mesh: f: 4 (over x), h: 32 (over z, y, core).
Axes of the slice: x: 4, y: 4, z: 4, core: 2. Of those that a mesh axis runs over, the one named last changes fastest.
Arguments:
- x: bfloat16 [4096, 4096], P(None, 'h')
- g1: float32 [4096], P('h')
- g2: float32 [4096], P('h')
- w_gate: bfloat16 [4096, 16384], P('h', 'f')
- w_up: bfloat16 [4096, 16384], P('h', 'f')
- w_down: bfloat16 [16384, 4096], P('f', 'h')
- o: bfloat16 [4096, 4096], P(None, 'f')
- w_o: bfloat16 [4096, 4096], P('f', 'h')
- w_qkv: bfloat16 [4096, 4608], P('h', 'f')
Outputs:
- output 1: bfloat16 [4096, 4096], P(None, 'h')
- output 2: bfloat16 [4096, 4608], P(None, 'f')
All inputs are finite; a program needn't handle non-finite values.
Results may differ from a plain program's by a relative error of at most 0.00392871.
Values are sent between devices in bfloat16 or wider.
A program may use at most 1 GiB of HBM per device.

v0:
```python
import jax
import jax.numpy as jnp
from jax import lax
from jax.sharding import PartitionSpec as P

EPS = 1e-6


def _dot(a, b):
    return jnp.dot(a, b, preferred_element_type=jnp.float32)


def _norm(x, g, d):
    xf = x.astype(jnp.float32)
    ss = lax.psum(jnp.sum(xf * xf, axis=-1, keepdims=True), 'h')
    r = lax.rsqrt(ss / d + EPS)
    return (xf * r * g).astype(jnp.bfloat16)


def solution(mesh):
    h = mesh.shape['h']

    def body(x, g1, g2, w_gate, w_up, w_down, o, w_o, w_qkv):
        d = x.shape[1] * h
        n = _norm(x, g1, d)
        gt, up = lax.psum((_dot(n, w_gate), _dot(n, w_up)), 'h')
        a = (jax.nn.silu(gt) * up).astype(jnp.bfloat16)
        y = lax.psum(_dot(a, w_down) + _dot(o, w_o), 'f')
        x_next = (x.astype(jnp.float32) + y).astype(jnp.bfloat16)
        n1 = _norm(x_next, g2, d)
        qkv = lax.psum(_dot(n1, w_qkv), 'h').astype(jnp.bfloat16)
        return x_next, qkv

    in_specs = (P(None, 'h'), P('h'), P('h'), P('h', 'f'), P('h', 'f'), P('f', 'h'),
                P(None, 'f'), P('f', 'h'), P('h', 'f'))
    return jax.shard_map(body, mesh=mesh, in_specs=in_specs,
                         out_specs=(P(None, 'h'), P(None, 'f')), check_vma=False)
```

profile of v0, /device:TPU:1, one launch (start us, length us, event | category | flops | bytes accessed | tf_op | source)
XLA Modules:
  0.0 1518.0 jit_solution(4800134070568285478)
XLA Ops:
  7.2 0.0 copy-start
  7.2 0.0 all-reduce.5.cloned.1.call-start
  7.2 1.9 fusion.5
  9.1 125.5 %psum.42 = f32[4096,1]{0,1:T(1,128)S(1)} all-reduce(f32[4096,1]{0,1:T(1,128)S(1)} %bitcast.14), channel_id=1, replica_groups=mesh['f'=4,'h'=32] {'h'}, use_global_device_ids=true, to_apply=%region_1.0 | all-reduce | flops 4096 | bytes 32768 | tf_op jit(solution)/shard_map/psum | solution.py:15
  134.7 0.0 copy-done
  134.7 24.3 %fusion.15 = f32[4096,4096]{1,0:T(8,128)} fusion(bf16[128,4096]{1,0:T(8,128)(2,1)S(1)} %copy-done, bf16[4096,128]{1,0:T(8,128)(2,1)} %param.9, f32[128]{0:T(128)} %param.10, f32[4096]{0:T(1024)S(1)} %bitcast.10), kind=kOutput, calls=%fused_computation.19 | convolution fusion | flops 4297064448 | bytes 69222912 | tf_op jit(solution)/shard_map/dot_general | solution.py:10
  159.0 0.0 all-reduce.5.cloned.1.call-update
  159.1 0.0 all-reduce.7.cloned.1.call-start
  159.1 1.1 copy-done.1
  160.3 0.3 copy-done.3
  160.6 0.0 copy-done.6
  160.6 24.2 %fusion.13 = f32[4096,4096]{1,0:T(8,128)} fusion(bf16[128,4096]{1,0:T(8,128)(2,1)S(1)} %copy-done.3, bf16[4096,128]{1,0:T(8,128)(2,1)S(1)} %copy-done.1, f32[128]{0:T(128)S(1)} %copy-done.6, f32[4096]{0:T(1024)S(1)} %bitcast.11), kind=kOutput, calls=%fused_computation.18 | convolution fusion | flops 4297064448 | bytes 69222912 | tf_op jit(solution)/shard_map/dot_general | solution.py:10
  184.8 0.0 all-reduce.7.cloned.1.call-update
  184.8 0.0 copy-start.8
  184.8 0.0 all-reduce.9.cloned.1.call-start
  184.9 0.9 copy-done.5
  185.7 7.0 fusion.19
  192.8 412.9 %all-reduce.5.cloned.1.call-done = f32[4096,4096]{1,0:T(8,128)} async-done(((f32[4096,4096]{1,0:T(8,128)}), f32[4096,4096]{1,0:T(8,128)}) %all-reduce.5.cloned.1.call-update) | async-done | bytes 67108880 | tf_op jit(solution)/shard_map/psum | solution.py:26
  605.6 449.4 %all-reduce.7.cloned.1.call-done = f32[4096,4096]{1,0:T(8,128)} async-done(((f32[4096,4096]{1,0:T(8,128)}), f32[4096,4096]{1,0:T(8,128)}) %all-reduce.7.cloned.1.call-update) | async-done | bytes 67108880 | tf_op jit(solution)/shard_map/psum | solution.py:26
  1055.0 0.0 copy-done.8
  1055.0 44.6 %fusion.1 = f32[4096,128]{1,0:T(8,128)} fusion(f32[4096,128]{1,0:T(8,128)} %fusion.19, bf16[4096,128]{1,0:T(8,128)(2,1)S(1)} %copy-done.8, f32[4096,4096]{1,0:T(8,128)} %all-reduce.7.cloned.1.call-done, f32[4096,4096]{1,0:T(8,128)} %all-reduce.5.cloned.1.call-done), kind=kOutput, calls=%fused_computation.2 | convolution fusion | flops 4396154880 | bytes 139460608 | tf_op jit(solution)/shard_map/dot_general | solution.py:10
  1099.6 0.0 all-reduce.9.cloned.1.call-update
  1099.6 0.0 copy-start.4
  1099.7 0.0 copy-start.7
  1099.7 58.3 %all-reduce.9.cloned.1.call-done = f32[4096,128]{1,0:T(8,128)} async-done(((f32[4096,128]{1,0:T(8,128)}), f32[4096,128]{1,0:T(8,128)}) %all-reduce.9.cloned.1.call-update) | async-done | bytes 2097168 | tf_op jit(solution)/shard_map/psum | solution.py:28
  1158.0 2.2 fusion.2
  1160.2 0.0 copy-start.2
  1160.2 123.3 %psum.46 = f32[4096,1]{0,1:T(1,128)S(1)} all-reduce(f32[4096,1]{0,1:T(1,128)S(1)} %bitcast.13), channel_id=1, replica_groups=mesh['f'=4,'h'=32] {'h'}, use_global_device_ids=true, to_apply=%region_6.7 | all-reduce | flops 4096 | bytes 32768 | tf_op jit(solution)/shard_map/psum | solution.py:15
  1283.6 0.0 copy-done.4
  1283.6 0.0 copy-done.7
  1283.6 7.9 fusion.9
  1291.5 219.9 %all-reduce.10 = bf16[4096,1152]{1,0:T(8,128)(2,1)} all-reduce(f32[4096,1152]{1,0:T(8,128)} %fusion.9), channel_id=1, replica_groups=mesh['f'=4,'h'=32] {'h'}, use_global_device_ids=true, to_apply=%region_7.8 | all-reduce | flops 4718592 | bytes 28311552 | tf_op jit(solution)/shard_map/psum | solution.py:31
  (7 shorter events, 0.1 us)
Async XLA Ops:
  7.2 127.5 %copy-start = (bf16[128,4096]{1,0:T(8,128)(2,1)S(1)}, bf16[128,4096]{1,0:T(8,128)(2,1)}, u32[]{:S(2)}) copy-start(bf16[128,4096]{1,0:T(8,128)(2,1)} %param.12) | copy-start | bytes 3145732
  7.2 598.5 %all-reduce.5.cloned.1.call-start = ((), (), s32[]{:S(2)}) async-start(), calls=%async_computation | async-start | bytes 134217728 | tf_op jit(solution)/shard_map/psum | solution.py:26
  159.0 1.2 copy-start.1
  159.0 1.5 copy-start.3
  159.0 1.5 copy-start.6
  159.1 896.0 %all-reduce.7.cloned.1.call-start = ((), (), s32[]{:S(2)}) async-start(), calls=%async_computation.1 | async-start | bytes 134217728 | tf_op jit(solution)/shard_map/psum | solution.py:26
  184.8 1.0 copy-start.5
  184.8 870.2 %copy-start.8 = (bf16[4096,128]{1,0:T(8,128)(2,1)S(1)}, bf16[4096,128]{1,0:T(8,128)(2,1)}, u32[]{:S(2)}) copy-start(bf16[4096,128]{1,0:T(8,128)(2,1)} %param.14) | copy-start | bytes 3145732
  184.8 973.2 %all-reduce.9.cloned.1.call-start = ((), (), s32[]{:S(2)}) async-start(), calls=%async_computation.2 | async-start | bytes 4194304 | tf_op jit(solution)/shard_map/psum | solution.py:28
  1099.6 183.9 %copy-start.4 = (bf16[128,1152]{1,0:T(8,128)(2,1)S(1)}, bf16[128,1152]{1,0:T(8,128)(2,1)}, u32[]{:S(2)}) copy-start(bf16[128,1152]{1,0:T(8,128)(2,1)} %param.17) | copy-start | bytes 884740
  1099.7 183.9 %copy-start.7 = (f32[128]{0:T(128)S(1)}, f32[128]{0:T(128)}, u32[]{:S(2)}) copy-start(f32[128]{0:T(128)} %param.11) | copy-start | bytes 1540
  1160.2 131.3 %copy-start.2 = (bf16[4096,128]{1,0:T(8,128)(2,1)}, bf16[4096,128]{1,0:T(8,128)(2,1)S(1)}, u32[]{:S(2)}) copy-start(bf16[4096,128]{1,0:T(8,128)(2,1)S(1)} %get-tuple-element.3) | copy-start | bytes 3145732
Sparse Core Ops, SparseCore 0:
  159.2 446.4 all-reduce.4
  609.6 445.3 all-reduce.6
  1099.8 58.1 all-reduce.8
where the time goes:
time: 1520 us
  waiting for transfers between devices  921 us (61%)
  blocking collectives  469 us (31%)
  matrix products  108 us (7%)
    psum x2, waiting for transfers between devices, body(): gt, up = lax.psum((_dot(n, w_gate), _dot(n, w_up)), 'h')  862 us
    psum x2, blocking collectives, _norm(): ss = lax.psum(jnp.sum(xf * xf, axis=-1, keepdims=True), 'h')  249 us
    psum x1, blocking collectives, body(): qkv = lax.psum(_dot(n1, w_qkv), 'h').astype(jnp.bfloat16)  220 us
    dot_general x5, matrix products, _dot(): return jnp.dot(a, b, preferred_element_type=jnp.float32)  108 us
    psum x1, waiting for transfers between devices, body(): y = lax.psum(_dot(a, w_down) + _dot(o, w_o), 'f')  58.3 us
  transfers between devices with their start and end apart: 3, of which 3 were waited for; matrix products, arithmetic and copies ran while one was open for 2% of the time, Pallas kernels for 0%

commit v1 on v0

v1 whole, which is shorter than its diff:
```python
import jax
import jax.numpy as jnp
from jax import lax
from jax.experimental import pallas as pl
from jax.experimental.pallas import tpu as pltpu
from jax.sharding import Mesh, PartitionSpec as P

EPS = 1e-6
MESH = pl.DeviceIdType.MESH
BF = jnp.bfloat16
F32 = jnp.float32
R = 4
B = 128
H = B // 2
Q = H // 2
D = 4096
DZ = D // R
DC = DZ // 2
NQ = 4
NP = 5
PK = NP * DZ
W = 1152
NSEND, NRECV, NLOC = 24, 120, 8


def _kernel(x5, g1, g2, wg, wu, wd, o, wo, wq, xo, qo,
            XR, XN, G1S, G2S, G1F, G2F, NF, WGU, AL, AF, OB, WD, PB, RB, XP, N2, N2B, WQ, QB, ss, rs, ls):
    x, y, z, c = (lax.axis_index(a) for a in "xyzc")
    here = {"x": x, "y": y, "z": z}

    def at(axis, d):
        return lax.rem(here[axis] + d, R)

    PLUS, MINUS, FAR = 1, R - 1, 2
    oc = 1 - c
    sib = {"c": oc}
    blk = y * 2 + c

    count = {"s": 0, "r": 0, "l": 0}
    limit = {"s": NSEND, "r": NRECV, "l": NLOC}

    def new(kind):
        count[kind] += 1
        assert count[kind] <= limit[kind]
        return count[kind] - 1

    sends = []

    class Sends:
        def __init__(self, ref):
            self.i, self.ref = new("s"), ref
            sends.append(self)

        def wait(self):
            pltpu.make_async_copy(self.ref, self.ref, ss.at[self.i]).wait()

    class Got:
        def __init__(self, ref):
            self.i, self.ref = new("r"), ref

        def wait(self, ref=None):
            ref = self.ref if ref is None else ref
            pltpu.make_async_copy(ref, ref, rs.at[self.i]).wait()

    def send(group, src, dst, dev, got):
        d = pltpu.make_async_remote_copy(
            src_ref=src, dst_ref=dst, send_sem=ss.at[group.i], recv_sem=rs.at[got.i],
            device_id=dev, device_id_type=MESH)
        d.start()

    def here_copy(src, dst, got):
        pltpu.make_async_copy(src, dst, rs.at[got.i]).start()

    def load(src, dst):
        d = pltpu.make_async_copy(src, dst, ls.at[new("l")])
        d.start()
        return d

    def span(b, n):
        return pl.ds(pl.multiple_of(b * n, n), n)

    def ahead(b, n, step):
        return pl.ds(pl.multiple_of(b, step), n)

    bar = pltpu.get_barrier_semaphore()
    peers = [(dx, dy, 0, 0) for dx in range(R) for dy in range(R) if dx + dy]
    peers += [(0, dy, 0, 1) for dy in range(R)]
    peers += [(0, 0, dz, dc) for dz in range(1, R) for dc in range(2)]
    for dx, dy, dz, dc in peers:
        pl.semaphore_signal(bar, inc=1, device_id={
            "x": at("x", dx), "y": at("y", dy), "z": at("z", dz), "c": oc if dc else c}, device_id_type=MESH)

    l_ob = load(o.at[span(z * 2 + c, DC), :], OB)
    l_wd = load(wd, WD.at[z, 0:D, span(c, B)])
    l_wo = load(wo, WD.at[z, D:PK, span(c, B)])
    l_wq = load(wq, WQ.at[z, blk])
    pl.semaphore_wait(bar, len(peers))

    near = [(dy, dc) for dy in (PLUS, MINUS, FAR, 0) for dc in range(2) if dy + dc]

    def yc(dy, dc):
        return at("y", dy), (oc if dc else c)

    firsts = ((x5, XR, XN), (g1, G1S, G1F), (g2, G2S, G2F))
    s1, s1s = [Got(b) for _, b, _ in firsts], [Sends(b.at[0:R - 1]) for _, b, _ in firsts]
    for dz in (PLUS, MINUS, FAR, 0):
        z2 = at("z", dz)
        for (src, dst, _), got, grp in zip(firsts, s1, s1s):
            s = src.at[z2, :, x] if src is x5 else src
            if dz:
                send(grp, s, dst.at[z], {"z": z2}, got)
            else:
                here_copy(s, dst.at[z], got)

    a2a, a2as = [Got(WGU.at[q, span(z, DZ), :]) for q in range(NQ)], Sends(NF.at[0:NQ * 7 * 8, :])

    def send_a2a(q):
        r = span(z * 8 + blk, B)
        for dy, dc in near + [(0, 0)]:
            y2, c2 = yc(dy, dc)
            cols = span((y2 * 2 + c2) * NQ + q, B)
            for w, off in ((wg, 0), (wu, B)):
                s, d = w.at[:, cols], WGU.at[q, r, off:off + B]
                if dy + dc:
                    send(a2as, s, d, {"y": y2, "c": c2}, a2a[q])
                else:
                    here_copy(s, d, a2a[q])

    class Ring:
        def __init__(self, axis, sends, own, half):
            self.axis, self.sends, self.half = axis, sends, half
            self.got = [Got(own), Got(own)]
            self.far = [Got(half(0, 0)), Got(half(0, 1))]

        def own(self, src, dst):
            for d, g in zip((PLUS, MINUS), self.got):
                send(self.sends, src, dst, {self.axis: at(self.axis, d)}, g)

        def wait(self):
            for g in self.got:
                g.wait()

        def onward(self):
            for h, (d, g) in enumerate(zip((PLUS, MINUS), self.far)):
                ref = self.half(at(self.axis, R - d), h)
                send(self.sends, ref, ref, {self.axis: at(self.axis, d)}, g)

        def wait_far(self):
            for g in self.far:
                g.wait()

    send_a2a(0)
    qz = Ring("z", Sends(WQ.at[0, 0:R - 1]), WQ.at[0, 0], lambda zz, h: WQ.at[zz, blk, h * H:h * H + H])
    qz.own(wq, WQ.at[z, blk])

    wds, wsib = Sends(WD.at[:, 0:PK * 7 // 8, :]), {}
    cuts = [(p, p * DZ, (p + 1) * DZ) for p in range(NP)]
    wgot = [[Got(WD.at[0, s:e, 0:B]), Got(WD.at[0, s:e, 0:B])] for _, s, e in cuts]
    wsib = [Got(WD.at[0, :, 0:B]) for _ in range(3)] + [Got(WD.at[0, :, 0:B])]
    wfar = []

    def w_own(p):
        _, s, e = cuts[p]
        src, dst = (wd.at[s:e, :] if e <= D else wo), WD.at[z, s:e, span(c, B)]
        for d, g in zip((PLUS, MINUS), wgot[p]):
            send(wds, src, dst, {"z": at("z", d)}, g)
        send(wds, src, dst, sib, wsib[0])

    def w_onward(p):
        _, s, e = cuts[p]
        for h, (d, g) in enumerate(zip((PLUS, MINUS), wgot[p])):
            g.wait()
            lo, hi = max(s, h * PK // 2), min(e, (h + 1) * PK // 2)
            zz = at("z", R - d)
            if lo < hi:
                ref = WD.at[zz, lo:hi, span(c, B)]
                got = Got(ref)
                send(wds, ref, ref, {"z": at("z", d)}, got)
                wfar.append((got, lo, hi))
            ref = WD.at[zz, s:e, span(c, B)]
            send(wds, ref, ref, sib, wsib[1 + h])

    for g in s1:
        g.wait()
    less = slice(0, 7 * B)
    s2, s2s = [Got(b.at[:, :, less]) for _, _, b in firsts], [Sends(b.at[:, :, less]) for _, _, b in firsts]
    for dy, dc in near:
        y2, c2 = yc(dy, dc)
        for (_, src, dst), got, grp in zip(firsts, s2, s2s):
            send(grp, src.at[:, c2] if src is XR else src, dst.at[:, :, span(blk, B)], {"y": y2, "c": c2}, got)
    for q in range(1, NQ):
        send_a2a(q)
    XN[:, :, span(blk, B)] = XR[:, c]
    G1F[:, :, span(blk, B)] = G1S[...]
    G2F[:, :, span(blk, B)] = G2S[...]

    zs = Sends(NF.at[0:NQ * R * (R - 1) * 16, :])
    zr = [Ring("z", zs, WGU.at[q, 0:DZ, :],
               lambda zz, h, q=q: WGU.at[q, span(zz * 2 + h, DC), :]) for q in range(NQ)]

    def z_own(q):
        a2a[q].wait()
        ref = WGU.at[q, span(z, DZ), :]
        zr[q].own(ref, ref)

    def z_onward(q):
        zr[q].wait()
        zr[q].onward()

    z_own(0)
    qz.wait()
    qz.onward()

    def norm(src, gain, dst, base, first, n):
        def step(i, _):
            r = span(first // 16 + i, 16)
            v = [src[k, r, :].astype(F32) for k in range(R)]
            s = sum(jnp.sum(t * t, axis=-1, keepdims=True) for t in v)
            inv = lax.rsqrt(s / D + EPS)
            for k in range(R):
                dst[ahead(base + i * 16, 16, 16), k * DZ:(k + 1) * DZ] = (v[k] * inv * gain[k]).astype(BF)
            return 0
        lax.fori_loop(0, n // 16, step, 0)

    for g in s2:
        g.wait()
    nrow = c * R + x
    norm(XN, G1F, NF, nrow * B, 0, B)

    def nhalf(xx, h):
        return NF.at[span((c * R + xx) * 2 + h, H), :]

    ns, nsib = Sends(NF.at[0:7 * B, :]), Got(NF.at[0:DC, :])
    xr = Ring("x", ns, NF.at[0:B, :], nhalf)

    def n_sib(xx):
        ref = NF.at[span(c * R + xx, B), :]
        send(ns, ref, ref, sib, nsib)

    ref = NF.at[span(nrow, B), :]
    xr.own(ref, ref)
    n_sib(x)
    z_own(1)
    z_onward(0)
    z_own(2)
    qz.wait_far()
    l_wq.wait()
    qys, qsib = Sends(WQ.at[:, 0:7]), Got(WQ.at[:, 0:R])
    qy = Ring("y", qys, WQ.at[:, 0], lambda yy, h: WQ.at[2 * h:2 * h + 2, yy * 2 + c])

    def q_sib(yy):
        ref = WQ.at[:, yy * 2 + c]
        send(qys, ref, ref, sib, qsib)

    qy.own(WQ.at[:, blk], WQ.at[:, blk])
    q_sib(y)
    xr.wait()
    xr.onward()
    n_sib(at("x", MINUS))
    n_sib(at("x", PLUS))
    z_onward(1)
    z_own(3)
    xr.wait_far()
    n_sib(at("x", FAR))
    z_onward(2)

    one = AF.at[:, :, 0:B]
    asend = Sends(AF.at[:, :, 0:NQ * 7 * B])
    agot = [[[Got(one), Got(one)] for _ in range(2)] for _ in range(NQ)]
    arest = Got(AF.at[:, :, 0:NQ * 3 * B])

    def act(q):
        def step(m, _):
            r = span(m, 256)
            gu = jnp.dot(NF[r, :], WGU[q], preferred_element_type=F32)
            g, u = gu[:, :B], gu[:, B:]
            AL[q, r, :] = (g * lax.logistic(g) * u).astype(BF)
            return 0
        lax.fori_loop(0, R, step, 0)
        col = span(blk * NQ + q, B)
        for i, d in enumerate((PLUS, MINUS)):
            for c2 in range(2):
                for c1 in range(2):
                    @pl.when(c == c1)
                    def _():
                        send(asend, AL4.at[q, c2], AF.at[:, :, col], {"y": at("y", d), "c": c2}, agot[q][i][c1])
        send(asend, AL4.at[q, oc], AF.at[:, :, col], sib, arest)
        AF[:, :, col] = AL4[q, c]

    def a_onward(q):
        for i, d in enumerate((PLUS, MINUS)):
            agot[q][i][i].wait()
            ref = AF.at[:, :, span((at("y", R - d) * 2 + i) * NQ + q, B)]
            send(asend, ref, ref, {"y": at("y", d)}, arest)

    def a_wait():
        for q in range(NQ):
            for i in range(2):
                agot[q][i][1 - i].wait()
        arest.wait()

    AL4 = AL.reshape(NQ, 2, R, B, B)
    nsib.wait()
    zr[0].wait_far()
    act(0)
    z_onward(3)
    for p in range(NP):
        w_own(p)
    zr[1].wait_far()
    act(1)
    a_onward(0)
    zr[2].wait_far()
    act(2)
    a_onward(1)
    zr[3].wait_far()
    act(3)
    a_onward(2)
    w_onward(0)
    a_onward(3)
    qy.wait()
    qy.onward()
    q_sib(at("y", MINUS))
    q_sib(at("y", PLUS))
    w_onward(1)
    l_ob.wait()
    l_wd.wait()
    l_wo.wait()

    zk = [z, at("z", MINUS), at("z", PLUS), at("z", FAR)]
    rsend, nsend = Sends(RB), Got
    rgot = [[Got(RB.at[k, :, 0:H]) for _ in range(2)] for k in range(R)]
    ngot = [Got(N2.at[:, 0:H]) for _ in range(2)]
    xgot, xsend = [Got(xo.at[0:7 * B]), Got(xo.at[0:24 * B])], Sends(xo.at[0:31 * B])
    nsend = new("s")

    def halves(h):
        return slice(h * H, h * H + H)

    def down(k, h):
        t = halves(h)
        a, oo = AF[:, t, :].reshape(2 * B, D), OB4[:, t, :].reshape(2 * B, DZ)
        p = (jnp.dot(a, WD[zk[k], 0:D, :], preferred_element_type=F32)
             + jnp.dot(oo, WD[zk[k], D:PK, :], preferred_element_type=F32))
        PB[k, :, t, :] = p.reshape(R, H, 2 * B)
        for d in (PLUS, MINUS, FAR):
            send(rsend, PB.at[k, at("x", d), t], RB.at[k, d - 1, t], {"x": at("x", d)}, rgot[k][h])

    OB4 = OB.reshape(R, B, DZ)

    def resid(k, h):
        t = halves(h)
        rgot[k][h].wait()
        yy = PB[k, x, t] + RB[k, 0, t] + RB[k, 1, t] + RB[k, 2, t]
        cols = span(y, 2 * B)
        XP[k, t] = (XN[zk[k], t, cols].astype(F32) + yy).astype(BF)
        dst = N2.at[zk[k], t, cols]
        for d in range(R):
            cp = pltpu.make_async_remote_copy(
                src_ref=XP.at[k, t], dst_ref=dst, send_sem=ss.at[nsend], recv_sem=rs.at[ngot[h].i],
                device_id={"x": at("x", d), "y": x}, device_id_type=MESH)
            if d:
                cp.start()
            else:
                pl.when(x != y)(cp.start)

                @pl.when(x == y)
                def _():
                    dst[...] = XP[k, t]

    def x_out(k):
        rows = xo.at[span((z * 2 + c) * R + x, B), :]
        send(xsend, XP.at[k, :, span(oc, B)], rows, {"z": zk[k], "c": oc}, xgot[0])
        if k:
            send(xsend, XP.at[k, :, span(c, B)], rows, {"z": zk[k]}, xgot[0])
        else:
            rows[...] = XP[k, :, span(c, B)]

    def x_onward():
        xgot[0].wait()
        ref = xo.reshape(R, 2, R, B, B).at[:, :, x]
        for d in (PLUS, MINUS, FAR):
            send(xsend, ref, ref, {"x": at("x", d)}, xgot[1])

    wdone = [0]

    def far(n):
        for g, s, e in wfar[wdone[0]:n]:
            g.wait()
            ref = WD.at[zk[3], s:e, span(c, B)]
            send(wds, ref, ref, sib, wsib[3])
        wdone[0] = n

    a_wait()
    wsib[0].wait()
    down(0, 0)
    down(0, 1)
    w_onward(2)
    w_onward(3)
    resid(0, 0)
    resid(0, 1)
    x_out(0)
    w_onward(4)
    wsib[1].wait()
    down(1, 0)
    down(1, 1)
    far(2)
    wsib[2].wait()
    down(2, 0)
    down(2, 1)
    far(4)
    resid(1, 0)
    resid(1, 1)
    x_out(1)
    qy.wait_far()
    q_sib(at("y", FAR))
    resid(2, 0)
    resid(2, 1)
    x_out(2)
    far(len(wfar))
    wsib[3].wait()
    down(3, 0)
    down(3, 1)
    resid(3, 0)
    resid(3, 1)
    x_out(3)
    qsib.wait()

    def qrow(zz, yy, off, n):
        return qo.at[ahead(((zz * 2 + c) * R + yy) * B + off, n, Q), :]

    osend, osib = Sends(qo.at[0:31 * B]), Got(qo.at[0:D // 2])

    def qkv(h):
        t = halves(h)

        @pl.when(x == y)
        def _():
            ngot[h].wait(N2.at[:, 0:H, 0:6 * B])

        @pl.when(x != y)
        def _():
            ngot[h].wait()
        norm(N2, G2F, N2B, h * H, h * H, H)
        for j in range(3):
            cols = slice(j * 3 * B, (j + 1) * 3 * B)
            w = WQ[:, :, :, cols].reshape(D, 3 * B)
            QB[t, cols] = jnp.dot(N2B[t, :], w, preferred_element_type=F32).astype(BF)
        qo[ahead(((z * 2 + c) * R + y) * B + h * H, H, H), :] = QB[t, :]

    def out_sib(ref):
        send(osend, ref, ref, sib, osib)

    class Fan:
        def __init__(self, h):
            first, second = "yz" if h == 0 else "zy"

            def block(i, j, off, n):
                a, b = at(first, i), at(second, j)
                return qrow(b if h == 0 else a, a if h == 0 else b, h * H + off, n)

            self.block, self.first, self.second = block, first, second
            whole, part = block(0, 0, 0, H), block(0, 0, 0, Q)
            self.f, self.ff = [Got(whole), Got(whole)], [Got(part), Got(part)]
            self.s = [[Got(whole), Got(whole)] for _ in range(3)] + [[Got(part), Got(part)] for _ in range(2)]
            self.last = Got(qo.at[0:2 * B])

        def both(self, axis, ref, gots):
            for d, g in zip((PLUS, MINUS), gots):
                send(osend, ref, ref, {axis: at(axis, d)}, g)

        def go(self):
            own = self.block(0, 0, 0, H)
            self.both(self.first, own, self.f)
            self.both(self.second, own, self.s[0])
            out_sib(own)
            yield
            for i, d in enumerate((PLUS, MINUS)):
                self.f[i].wait()
                ref = self.block(R - d, 0, i * Q, Q)
                send(osend, ref, ref, {self.first: at(self.first, d)}, self.ff[i])
                ref = self.block(R - d, 0, 0, H)
                self.both(self.second, ref, self.s[1 + i])
                out_sib(ref)
            yield
            for i in range(2):
                self.ff[i].wait()
                ref = self.block(FAR, 0, i * Q, Q)
                self.both(self.second, ref, self.s[3 + i])
                out_sib(ref)
            yield
            for i, p in enumerate((0, MINUS, PLUS)):
                for u, d in enumerate((PLUS, MINUS)):
                    self.s[i][u].wait()
                    ref = self.block(p, R - d, u * Q, Q)
                    send(osend, ref, ref, {self.second: at(self.second, d)}, self.last)
                    out_sib(self.block(p, R - d, 0, H))
                yield
            for i in range(2):
                for u, d in enumerate((PLUS, MINUS)):
                    self.s[3 + i][u].wait()
                    ref = self.block(FAR, R - d, i * Q, Q)
                    if i == u:
                        send(osend, ref, ref, {self.second: at(self.second, d)}, self.last)
                    out_sib(ref)
            yield
            self.last.wait()
            for p in range(R):
                out_sib(self.block(p, FAR, 0, H))
            yield

    fans = []
    for h in range(2):
        qkv(h)
        fans.append(Fan(h).go())
        next(fans[h])
    for i, _ in enumerate(zip(*fans)):
        if i == 0:
            x_onward()
    osib.wait()
    xgot[1].wait()
    for s in sends:
        s.wait()

    @pl.when(x == y)
    def _():
        r = N2.at[:, :, 0:6 * B]
        pltpu.make_async_copy(r, r, ss.at[nsend]).wait()

    @pl.when(x != y)
    def _():
        pltpu.make_async_copy(N2, N2, ss.at[nsend]).wait()


def solution(mesh):
    mesh4 = Mesh(mesh.devices.reshape(R, R, R, 2), ("x", "z", "y", "c"))

    def body(x, g1, g2, w_gate, w_up, w_down, o, w_o, w_qkv):
        vm = pltpu.VMEM
        anyspec = pl.BlockSpec(memory_space=pl.ANY)
        sem = pltpu.SemaphoreType.DMA
        return pl.pallas_call(
            _kernel,
            out_shape=(vm((D, B), BF), vm((D, W), BF)),
            in_specs=[anyspec] * 9,
            out_specs=(pl.BlockSpec(memory_space=vm), pl.BlockSpec(memory_space=vm)),
            scratch_shapes=[
                vm((R, 2, B, B), BF),
                vm((R, B, DZ), BF),
                vm((R, 1, B), F32), vm((R, 1, B), F32),
                vm((R, 1, DZ), F32), vm((R, 1, DZ), F32),
                vm((DZ, D), BF),
                vm((NQ, D, 2 * B), BF),
                vm((NQ, DZ, B), BF),
                vm((R, B, D), BF),
                vm((DC, DZ), BF),
                vm((R, PK, 2 * B), BF),
                vm((R, R, B, 2 * B), F32),
                vm((R, R - 1, B, 2 * B), F32),
                vm((R, B, 2 * B), BF),
                vm((R, B, DZ), BF),
                vm((B, D), BF),
                vm((R, 8, B, W), BF),
                vm((B, W), BF),
                sem((NSEND,)), sem((NRECV,)), sem((NLOC,)),
            ],
            compiler_params=pltpu.CompilerParams(
                collective_id=0, has_side_effects=True, vmem_limit_bytes=50 * 2**20),
            name="block",
        )(x.reshape(R, 2, R, B, B), g1.reshape(1, B), g2.reshape(1, B), w_gate, w_up, w_down, o, w_o, w_qkv)

    h = ("z", "y", "c")
    in_specs = (P(None, h), P(h), P(h), P(h, "x"), P(h, "x"), P("x", h), P(None, "x"), P("x", h), P(h, "x"))
    return jax.shard_map(body, mesh=mesh4, in_specs=in_specs, out_specs=(P(None, h), P(None, "x")), check_vma=False)
```

time: 1520 us -> 196 us (0.13)
  waiting for transfers between devices: 921 us -> 0 us
  blocking collectives: 469 us -> 0 us
  Pallas kernels: 0 us -> 191 us
  matrix products: 108 us -> 0 us
    psum x3 -> x0, waiting for transfers between devices: 921 us -> none  [the longest x2 862 us: body(): gt, up = lax.psum((_dot(n, w_gate), _dot(n, w_up)), 'h')]
    psum x3 -> x0, blocking collectives: 469 us -> none  [the longest x2 249 us: _norm(): ss = lax.psum(jnp.sum(xf * xf, axis=-1, keepdims=True), 'h')]
    pallas_call x0 -> x1, Pallas kernels: none -> 191 us  [body(): pl.pallas_call(_kernel, out_shape=(vm((D, B), BF), vm((D, W), BF)), in_sp...]
    dot_general x5 -> x0, matrix products: 108 us -> none  [_dot(): return jnp.dot(a, b, preferred_element_type=jnp.float32)]
  transfers between devices with their start and end apart: 3 -> 0, of which waited for: 3 -> 0; matrix products, arithmetic and copies ran while one was open for 2% -> 0% of each run, Pallas kernels for 0% -> 0%
where the time goes in v1:
time: 196 us
  Pallas kernels  191 us (97%)
  local copies, waits for them, and re-layouts  4.71 us (2%)
    pallas_call x1, Pallas kernels, body(): pl.pallas_call(_kernel, out_shape=(vm((D, B), BF), vm((D, W), BF)), in_sp...  191 us
    unnamed x2, local copies, waits for them, and re-layouts  4.71 us

profile of v1, /device:TPU:1, one launch (start us, length us, event | category | flops | bytes accessed | tf_op | source)
XLA Modules:
  0.0 195.9 jit_solution(17696929032374682952)
XLA Ops:
  0.6 190.5 %block.1 = (bf16[4096,128]{1,0:T(8,128)(2,1)S(1)}, bf16[4096,1152]{1,0:T(8,128)(2,1)S(1)}) custom-call(bf16[4,2,4,128,128]{4,3,2,1,0:T(8,128)(2,1)} %bitcast.3, f32[1,128]{1,0:T(1,128)} %bitcast.4, f32[1,128]{1,0:T(1,128)} %bitcast.5, bf16[128,4096]{1,0:T(8,128)(2,1)} %wg.1, bf16[128,4096]{1,0:T(8,128)(2,1)} %wu.1, bf16[4096,128]{1,0:T(8,128)(2,1)} %wd.1, ...), custom_call_target="tpu_custom_call" | custom-call | tf_op jit(solution)/shard_map/block/pallas_call | solution.py:541
  191.1 1.0 copy.13
  192.1 3.7 %copy.14 = bf16[4096,1152]{1,0:T(8,128)(2,1)} copy(bf16[4096,1152]{1,0:T(8,128)(2,1)S(1)} %get-tuple-element.3) | data formatting | bytes 18874368

commit v2 on v1

--- a/solution.py
+++ b/solution.py
@@ -20,7 +20,7 @@
 NP = 5
 PK = NP * DZ
 W = 1152
-NSEND, NRECV, NLOC = 24, 120, 8
+NSEND, NRECV, NLOC = 24, 172, 12
 
 
 def _kernel(x5, g1, g2, wg, wu, wd, o, wo, wq, xo, qo,
@@ -90,7 +90,8 @@
         pl.semaphore_signal(bar, inc=1, device_id={
             "x": at("x", dx), "y": at("y", dy), "z": at("z", dz), "c": oc if dc else c}, device_id_type=MESH)
 
-    l_ob = load(o.at[span(z * 2 + c, DC), :], OB)
+    DIST = (0, PLUS, MINUS, FAR)
+    l_ob = [load(o.at[span((z * 2 + c) * R + at("x", d), B), :], OB.at[i]) for i, d in enumerate(DIST)]
     l_wd = load(wd, WD.at[z, 0:D, span(c, B)])
     l_wo = load(wo, WD.at[z, D:PK, span(c, B)])
     l_wq = load(wq, WQ.at[z, blk])
@@ -150,6 +151,7 @@
                 g.wait()
 
     send_a2a(0)
+    send_a2a(1)
     qz = Ring("z", Sends(WQ.at[0, 0:R - 1]), WQ.at[0, 0], lambda zz, h: WQ.at[zz, blk, h * H:h * H + H])
     qz.own(wq, WQ.at[z, blk])
 
@@ -188,7 +190,7 @@
         y2, c2 = yc(dy, dc)
         for (_, src, dst), got, grp in zip(firsts, s2, s2s):
             send(grp, src.at[:, c2] if src is XR else src, dst.at[:, :, span(blk, B)], {"y": y2, "c": c2}, got)
-    for q in range(1, NQ):
+    for q in range(2, NQ):
         send_a2a(q)
     XN[:, :, span(blk, B)] = XR[:, c]
     G1F[:, :, span(blk, B)] = G1S[...]
@@ -208,6 +210,7 @@
         zr[q].onward()
 
     z_own(0)
+    z_own(1)
     qz.wait()
     qz.onward()
 
@@ -230,17 +233,16 @@
     def nhalf(xx, h):
         return NF.at[span((c * R + xx) * 2 + h, H), :]
 
-    ns, nsib = Sends(NF.at[0:7 * B, :]), Got(NF.at[0:DC, :])
+    ns, nsib = Sends(NF.at[0:7 * B, :]), [Got(NF.at[0:3 * B, :]), Got(NF.at[0:B, :])]
     xr = Ring("x", ns, NF.at[0:B, :], nhalf)
 
-    def n_sib(xx):
+    def n_sib(xx, got):
         ref = NF.at[span(c * R + xx, B), :]
-        send(ns, ref, ref, sib, nsib)
+        send(ns, ref, ref, sib, got)
 
     ref = NF.at[span(nrow, B), :]
     xr.own(ref, ref)
-    n_sib(x)
-    z_own(1)
+    n_sib(x, nsib[0])
     z_onward(0)
     z_own(2)
     qz.wait_far()
@@ -252,77 +254,88 @@
         ref = WQ.at[:, yy * 2 + c]
         send(qys, ref, ref, sib, qsib)
 
-    qy.own(WQ.at[:, blk], WQ.at[:, blk])
+    def q_own(h):
+        ref = WQ.at[2 * h:2 * h + 2, blk]
+        qy.own(ref, ref)
+
+    q_own(0)
     q_sib(y)
+    z_onward(1)
+    z_own(3)
     xr.wait()
     xr.onward()
-    n_sib(at("x", MINUS))
-    n_sib(at("x", PLUS))
-    z_onward(1)
-    z_own(3)
-    xr.wait_far()
-    n_sib(at("x", FAR))
-    z_onward(2)
-
-    one = AF.at[:, :, 0:B]
+    n_sib(at("x", MINUS), nsib[0])
+    n_sib(at("x", PLUS), nsib[0])
+
+    units = [[(0, 0, 3)], [(1, 0, 3)], [(0, 3, R), (1, 3, R)], [(2, 0, R)], [(3, 0, R)]]
     asend = Sends(AF.at[:, :, 0:NQ * 7 * B])
-    agot = [[[Got(one), Got(one)] for _ in range(2)] for _ in range(NQ)]
     arest = Got(AF.at[:, :, 0:NQ * 3 * B])
-
-    def act(q):
-        def step(m, _):
-            r = span(m, 256)
-            gu = jnp.dot(NF[r, :], WGU[q], preferred_element_type=F32)
-            g, u = gu[:, :B], gu[:, B:]
-            AL[q, r, :] = (g * lax.logistic(g) * u).astype(BF)
-            return 0
-        lax.fori_loop(0, R, step, 0)
-        col = span(blk * NQ + q, B)
+    agot = []
+    for u in units:
+        n = AF.at[0:sum(hi - lo for _, lo, hi in u), :, 0:B]
+        agot.append([[Got(n), Got(n)] for _ in range(2)])
+    NF4 = NF.reshape(2, R, B, D)
+
+    def act(u):
+        for q, lo, hi in units[u]:
+            def step(s, _):
+                xb = at("x", s + s // 2 - s // 3 * 2)
+                gu = jnp.dot(NF4[:, xb].reshape(2 * B, D), WGU[q], preferred_element_type=F32)
+                g, up = gu[:, :B], gu[:, B:]
+                AL[q, :, s] = (g * lax.logistic(g) * up).astype(BF).reshape(2, B, B)
+                return 0
+            lax.fori_loop(lo, hi, step, 0)
+            col = span(blk * NQ + q, B)
+            dst = AF.at[lo:hi, :, col]
+            for i, d in enumerate((PLUS, MINUS)):
+                for c2 in range(2):
+                    for c1 in range(2):
+                        @pl.when(c == c1)
+                        def _():
+                            send(asend, AL.at[q, c2, lo:hi], dst, {"y": at("y", d), "c": c2}, agot[u][i][c1])
+            send(asend, AL.at[q, oc, lo:hi], dst, sib, arest)
+            AF[lo:hi, :, col] = AL[q, c, lo:hi]
+
+    def a_onward(u):
         for i, d in enumerate((PLUS, MINUS)):
-            for c2 in range(2):
-                for c1 in range(2):
-                    @pl.when(c == c1)
-                    def _():
-                        send(asend, AL4.at[q, c2], AF.at[:, :, col], {"y": at("y", d), "c": c2}, agot[q][i][c1])
-        send(asend, AL4.at[q, oc], AF.at[:, :, col], sib, arest)
-        AF[:, :, col] = AL4[q, c]
-
-    def a_onward(q):
-        for i, d in enumerate((PLUS, MINUS)):
-            agot[q][i][i].wait()
-            ref = AF.at[:, :, span((at("y", R - d) * 2 + i) * NQ + q, B)]
-            send(asend, ref, ref, {"y": at("y", d)}, arest)
+            agot[u][i][i].wait()
+            for q, lo, hi in units[u]:
+                ref = AF.at[lo:hi, :, span((at("y", R - d) * 2 + i) * NQ + q, B)]
+                send(asend, ref, ref, {"y": at("y", d)}, arest)
 
     def a_wait():
-        for q in range(NQ):
+        for u in range(len(units)):
             for i in range(2):
-                agot[q][i][1 - i].wait()
+                agot[u][i][1 - i].wait()
         arest.wait()
 
-    AL4 = AL.reshape(NQ, 2, R, B, B)
-    nsib.wait()
+    nsib[0].wait()
     zr[0].wait_far()
     act(0)
+    z_onward(2)
+    zr[1].wait_far()
+    act(1)
+    xr.wait_far()
+    n_sib(at("x", FAR), nsib[1])
+    a_onward(0)
+    nsib[1].wait()
+    act(2)
+    a_onward(1)
     z_onward(3)
     for p in range(NP):
         w_own(p)
-    zr[1].wait_far()
-    act(1)
-    a_onward(0)
+    a_onward(2)
     zr[2].wait_far()
-    act(2)
-    a_onward(1)
+    act(3)
     zr[3].wait_far()
-    act(3)
-    a_onward(2)
+    act(4)
+    a_onward(3)
     w_onward(0)
-    a_onward(3)
-    qy.wait()
-    qy.onward()
-    q_sib(at("y", MINUS))
-    q_sib(at("y", PLUS))
+    a_onward(4)
+    q_own(1)
     w_onward(1)
-    l_ob.wait()
+    for d in l_ob:
+        d.wait()
     l_wd.wait()
     l_wo.wait()
 
@@ -338,19 +351,18 @@
 
     def down(k, h):
         t = halves(h)
-        a, oo = AF[:, t, :].reshape(2 * B, D), OB4[:, t, :].reshape(2 * B, DZ)
+        a, oo = AF[:, t, :].reshape(2 * B, D), OB[:, t, :].reshape(2 * B, DZ)
         p = (jnp.dot(a, WD[zk[k], 0:D, :], preferred_element_type=F32)
              + jnp.dot(oo, WD[zk[k], D:PK, :], preferred_element_type=F32))
         PB[k, :, t, :] = p.reshape(R, H, 2 * B)
-        for d in (PLUS, MINUS, FAR):
-            send(rsend, PB.at[k, at("x", d), t], RB.at[k, d - 1, t], {"x": at("x", d)}, rgot[k][h])
-
-    OB4 = OB.reshape(R, B, DZ)
+        for i, d in enumerate(DIST):
+            if i:
+                send(rsend, PB.at[k, i, t], RB.at[k, i - 1, t], {"x": at("x", d)}, rgot[k][h])
 
     def resid(k, h):
         t = halves(h)
         rgot[k][h].wait()
-        yy = PB[k, x, t] + RB[k, 0, t] + RB[k, 1, t] + RB[k, 2, t]
+        yy = PB[k, 0, t] + RB[k, 0, t] + RB[k, 1, t] + RB[k, 2, t]
         cols = span(y, 2 * B)
         XP[k, t] = (XN[zk[k], t, cols].astype(F32) + yy).astype(BF)
         dst = N2.at[zk[k], t, cols]
@@ -384,7 +396,8 @@
     wdone = [0]
 
     def far(n):
-        for g, s, e in wfar[wdone[0]:n]:
+        order = [wfar[i] for t in range(len(wfar) // 2) for i in (t, t + len(wfar) // 2)]
+        for g, s, e in order[wdone[0]:n]:
             g.wait()
             ref = WD.at[zk[3], s:e, span(c, B)]
             send(wds, ref, ref, sib, wsib[3])
@@ -397,29 +410,34 @@
     w_onward(2)
     w_onward(3)
     resid(0, 0)
-    resid(0, 1)
-    x_out(0)
     w_onward(4)
     wsib[1].wait()
     down(1, 0)
     down(1, 1)
-    far(2)
+    resid(0, 1)
+    x_out(0)
+    qy.wait()
+    qy.onward()
+    q_sib(at("y", MINUS))
+    q_sib(at("y", PLUS))
     wsib[2].wait()
     down(2, 0)
     down(2, 1)
-    far(4)
+    far(2)
     resid(1, 0)
     resid(1, 1)
     x_out(1)
-    qy.wait_far()
-    q_sib(at("y", FAR))
+    far(3)
     resid(2, 0)
+    far(4)
     resid(2, 1)
     x_out(2)
     far(len(wfar))
     wsib[3].wait()
     down(3, 0)
     down(3, 1)
+    qy.wait_far()
+    q_sib(at("y", FAR))
     resid(3, 0)
     resid(3, 1)
     x_out(3)
@@ -450,72 +468,69 @@
     def out_sib(ref):
         send(osend, ref, ref, sib, osib)
 
-    class Fan:
-        def __init__(self, h):
-            first, second = "yz" if h == 0 else "zy"
-
-            def block(i, j, off, n):
-                a, b = at(first, i), at(second, j)
-                return qrow(b if h == 0 else a, a if h == 0 else b, h * H + off, n)
-
-            self.block, self.first, self.second = block, first, second
-            whole, part = block(0, 0, 0, H), block(0, 0, 0, Q)
-            self.f, self.ff = [Got(whole), Got(whole)], [Got(part), Got(part)]
-            self.s = [[Got(whole), Got(whole)] for _ in range(3)] + [[Got(part), Got(part)] for _ in range(2)]
-            self.last = Got(qo.at[0:2 * B])
-
-        def both(self, axis, ref, gots):
-            for d, g in zip((PLUS, MINUS), gots):
-                send(osend, ref, ref, {axis: at(axis, d)}, g)
-
-        def go(self):
-            own = self.block(0, 0, 0, H)
-            self.both(self.first, own, self.f)
-            self.both(self.second, own, self.s[0])
-            out_sib(own)
-            yield
-            for i, d in enumerate((PLUS, MINUS)):
-                self.f[i].wait()
-                ref = self.block(R - d, 0, i * Q, Q)
-                send(osend, ref, ref, {self.first: at(self.first, d)}, self.ff[i])
-                ref = self.block(R - d, 0, 0, H)
-                self.both(self.second, ref, self.s[1 + i])
-                out_sib(ref)
-            yield
-            for i in range(2):
-                self.ff[i].wait()
-                ref = self.block(FAR, 0, i * Q, Q)
-                self.both(self.second, ref, self.s[3 + i])
-                out_sib(ref)
-            yield
-            for i, p in enumerate((0, MINUS, PLUS)):
+    todo = {}
+
+    def coming(name, ref, then, whole):
+        todo[name] = (Got(ref), then, whole)
+
+    def fan(h):
+        first, second = "yz" if h == 0 else "zy"
+
+        def block(i, j, off, n):
+            a, b = at(first, i), at(second, j)
+            return qrow(b if h == 0 else a, a if h == 0 else b, h * H + off, n)
+
+        def hop(axis, d, ref, name):
+            send(osend, ref, ref, {axis: at(axis, d)}, todo[name][0])
+
+        def across(name, i, parts):
+            def start():
+                for off, n, part in parts:
+                    for d in (PLUS, MINUS):
+                        hop(second, d, block(i, 0, off, n), f"s{h}{name}{part}{d}")
+            for off, n, part in parts:
                 for u, d in enumerate((PLUS, MINUS)):
-                    self.s[i][u].wait()
-                    ref = self.block(p, R - d, u * Q, Q)
-                    send(osend, ref, ref, {self.second: at(self.second, d)}, self.last)
-                    out_sib(self.block(p, R - d, 0, H))
-                yield
-            for i in range(2):
-                for u, d in enumerate((PLUS, MINUS)):
-                    self.s[3 + i][u].wait()
-                    ref = self.block(FAR, R - d, i * Q, Q)
-                    if i == u:
-                        send(osend, ref, ref, {self.second: at(self.second, d)}, self.last)
-                    out_sib(ref)
-            yield
-            self.last.wait()
-            for p in range(R):
-                out_sib(self.block(p, FAR, 0, H))
-            yield
-
-    fans = []
+                    def onward(u=u, d=d, off=off, part=part):
+                        if part in ("", str(u)):
+                            hop(second, d, block(i, R - d, u * Q, Q), f"l{h}{name}{u}")
+                    coming(f"s{h}{name}{part}{d}", block(i, R - d, off, n), onward, block(i, R - d, off, n))
+            for u in range(2):
+                ref = block(i, FAR, u * Q, Q)
+                coming(f"l{h}{name}{u}", ref, None, ref)
+            return start
+
+        full = [(0, H, "")]
+        go = {name: across(name, i, full) for name, i in (("o", 0), ("m", MINUS), ("p", PLUS))}
+        far = across("f", FAR, [(0, Q, "0"), (Q, Q, "1")])
+        for u, (d, name) in enumerate(((PLUS, "m"), (MINUS, "p"))):
+            def onward(u=u, d=d, name=name):
+                hop(first, d, block(R - d, 0, u * Q, Q), f"r{h}{u}")
+                go[name]()
+            coming(f"f{h}{d}", block(R - d, 0, 0, H), onward, block(R - d, 0, 0, H))
+            ref = block(FAR, 0, u * Q, Q)
+
+            def rest(u=u):
+                for d in (PLUS, MINUS):
+                    hop(second, d, block(FAR, 0, u * Q, Q), f"s{h}f{u}{d}")
+            coming(f"r{h}{u}", ref, rest, ref)
+        own = block(0, 0, 0, H)
+        for d in (PLUS, MINUS):
+            hop(first, d, own, f"f{h}{d}")
+        go["o"]()
+        out_sib(own)
+
     for h in range(2):
         qkv(h)
-        fans.append(Fan(h).go())
-        next(fans[h])
-    for i, _ in enumerate(zip(*fans)):
-        if i == 0:
-            x_onward()
+        fan(h)
+    x_onward()
+    for key in "f0 s0o s1o f1 r0 s0m l1o s0p s1m l0o r1 s1p s0f0 l1m s0f1 s1f0 l0m s1f1 l0p l1p l0f l1f".split():
+        for name in [n for n in todo if n.startswith(key)]:
+            got, then, ref = todo.pop(name)
+            got.wait()
+            if then:
+                then()
+            out_sib(ref)
+    assert not todo
     osib.wait()
     xgot[1].wait()
     for s in sends:
@@ -550,9 +565,9 @@
                 vm((R, 1, DZ), F32), vm((R, 1, DZ), F32),
                 vm((DZ, D), BF),
                 vm((NQ, D, 2 * B), BF),
-                vm((NQ, DZ, B), BF),
+                vm((NQ, 2, R, B, B), BF),
                 vm((R, B, D), BF),
-                vm((DC, DZ), BF),
+                vm((R, B, DZ), BF),
                 vm((R, PK, 2 * B), BF),
                 vm((R, R, B, 2 * B), F32),
                 vm((R, R - 1, B, 2 * B), F32),

time: 196 us -> 189 us (0.964)
  Pallas kernels: 191 us -> 184 us
    pallas_call x1, Pallas kernels: 191 us -> 184 us  [body(): pl.pallas_call(_kernel, out_shape=(vm((D, B), BF), vm((D, W), BF)), in_sp...]
where the time goes in v2:
time: 189 us
  Pallas kernels  184 us (97%)
  local copies, waits for them, and re-layouts  4.71 us (2%)
    pallas_call x1, Pallas kernels, body(): pl.pallas_call(_kernel, out_shape=(vm((D, B), BF), vm((D, W), BF)), in_sp...  184 us
    unnamed x2, local copies, waits for them, and re-layouts  4.71 us

profile of v2, /device:TPU:1, one launch (start us, length us, event | category | flops | bytes accessed | tf_op | source)
XLA Modules:
  0.0 189.0 jit_solution(14501875760524874213)
XLA Ops:
  0.6 183.6 %block.1 = (bf16[4096,128]{1,0:T(8,128)(2,1)S(1)}, bf16[4096,1152]{1,0:T(8,128)(2,1)S(1)}) custom-call(bf16[4,2,4,128,128]{4,3,2,1,0:T(8,128)(2,1)} %bitcast.3, f32[1,128]{1,0:T(1,128)} %bitcast.4, f32[1,128]{1,0:T(1,128)} %bitcast.5, bf16[128,4096]{1,0:T(8,128)(2,1)} %wg.1, bf16[128,4096]{1,0:T(8,128)(2,1)} %wu.1, bf16[4096,128]{1,0:T(8,128)(2,1)} %wd.1, ...), custom_call_target="tpu_custom_call" | custom-call | tf_op jit(solution)/shard_map/block/pallas_call | solution.py:556
  184.3 1.0 copy.13
  185.2 3.7 %copy.14 = bf16[4096,1152]{1,0:T(8,128)(2,1)} copy(bf16[4096,1152]{1,0:T(8,128)(2,1)S(1)} %get-tuple-element.3) | data formatting | bytes 18874368

commit v3 on v2

--- a/solution.py
+++ b/solution.py
@@ -17,14 +17,14 @@
 DZ = D // R
 DC = DZ // 2
 NQ = 4
-NP = 5
-PK = NP * DZ
+NP = 4
 W = 1152
-NSEND, NRECV, NLOC = 24, 172, 12
+NSEND, NRECV, NLOC = 30, 200, 20
 
 
 def _kernel(x5, g1, g2, wg, wu, wd, o, wo, wq, xo, qo,
-            XR, XN, G1S, G2S, G1F, G2F, NF, WGU, AL, AF, OB, WD, PB, RB, XP, N2, N2B, WQ, QB, ss, rs, ls):
+            XR, XN, G1S, G2S, G1F, G2F, NF, WGU, AL, AF, OT, WO, OR, OS, OD, WD, PB, RB, XP, N2, N2B, WQ,
+            ss, rs, ls):
     x, y, z, c = (lax.axis_index(a) for a in "xyzc")
     here = {"x": x, "y": y, "z": z}
 
@@ -91,9 +91,12 @@
             "x": at("x", dx), "y": at("y", dy), "z": at("z", dz), "c": oc if dc else c}, device_id_type=MESH)
 
     DIST = (0, PLUS, MINUS, FAR)
-    l_ob = [load(o.at[span((z * 2 + c) * R + at("x", d), B), :], OB.at[i]) for i, d in enumerate(DIST)]
-    l_wd = load(wd, WD.at[z, 0:D, span(c, B)])
-    l_wo = load(wo, WD.at[z, D:PK, span(c, B)])
+    l_wo = load(wo, WO)
+    NT = D // (2 * B)
+    tiles = [pltpu.make_async_copy(o.at[i * 2 * B:(i + 1) * 2 * B, :], OT.at[i % R], ls.at[new("l")]) for i in range(NT)]
+    for i in range(R):
+        tiles[i].start()
+    l_wd = load(wd, WD.at[z, :, span(c, B)])
     l_wq = load(wq, WQ.at[z, blk])
     pl.semaphore_wait(bar, len(peers))
 
@@ -155,7 +158,7 @@
     qz = Ring("z", Sends(WQ.at[0, 0:R - 1]), WQ.at[0, 0], lambda zz, h: WQ.at[zz, blk, h * H:h * H + H])
     qz.own(wq, WQ.at[z, blk])
 
-    wds, wsib = Sends(WD.at[:, 0:PK * 7 // 8, :]), {}
+    wds = Sends(WD.at[:, 0:D * 7 // 8, :])
     cuts = [(p, p * DZ, (p + 1) * DZ) for p in range(NP)]
     wgot = [[Got(WD.at[0, s:e, 0:B]), Got(WD.at[0, s:e, 0:B])] for _, s, e in cuts]
     wsib = [Got(WD.at[0, :, 0:B]) for _ in range(3)] + [Got(WD.at[0, :, 0:B])]
@@ -163,7 +166,7 @@
 
     def w_own(p):
         _, s, e = cuts[p]
-        src, dst = (wd.at[s:e, :] if e <= D else wo), WD.at[z, s:e, span(c, B)]
+        src, dst = wd.at[s:e, :], WD.at[z, s:e, span(c, B)]
         for d, g in zip((PLUS, MINUS), wgot[p]):
             send(wds, src, dst, {"z": at("z", d)}, g)
         send(wds, src, dst, sib, wsib[0])
@@ -172,7 +175,7 @@
         _, s, e = cuts[p]
         for h, (d, g) in enumerate(zip((PLUS, MINUS), wgot[p])):
             g.wait()
-            lo, hi = max(s, h * PK // 2), min(e, (h + 1) * PK // 2)
+            lo, hi = max(s, h * D // 2), min(e, (h + 1) * D // 2)
             zz = at("z", R - d)
             if lo < hi:
                 ref = WD.at[zz, lo:hi, span(c, B)]
@@ -182,6 +185,17 @@
             ref = WD.at[zz, s:e, span(c, B)]
             send(wds, ref, ref, sib, wsib[1 + h])
 
+    l_wo.wait()
+    os, og = Sends(OR), Got(OR)
+    for i in range(NT):
+        tiles[i].wait()
+        p, q, r = i // 2 // 2, i // 2 % 2, i % 2 * 2
+        PB[p, q, r:r + 2] = jnp.dot(OT[i % R], WO[...], preferred_element_type=F32).reshape(2, B, B)
+        if i + R < NT:
+            tiles[i + R].start()
+        if q and r:
+            for j, d in enumerate((PLUS, MINUS, FAR)):
+                send(os, PB.at[p, :, at("x", d)], OR.at[j, p], {"x": at("x", d)}, og)
     for g in s1:
         g.wait()
     less = slice(0, 7 * B)
@@ -248,24 +262,53 @@
     qz.wait_far()
     l_wq.wait()
     qys, qsib = Sends(WQ.at[:, 0:7]), Got(WQ.at[:, 0:R])
-    qy = Ring("y", qys, WQ.at[:, 0], lambda yy, h: WQ.at[2 * h:2 * h + 2, yy * 2 + c])
-
-    def q_sib(yy):
-        ref = WQ.at[:, yy * 2 + c]
+    slab = WQ.at[0, 0]
+    qgot = [[Got(slab), Got(slab)] for _ in range(R)]
+    qfar = [Got(slab) for _ in range(R)]
+
+    def q_own(j):
+        ref = WQ.at[j, blk]
+        for d, g in zip((PLUS, MINUS), qgot[j]):
+            send(qys, ref, ref, {"y": at("y", d)}, g)
         send(qys, ref, ref, sib, qsib)
 
-    def q_own(h):
-        ref = WQ.at[2 * h:2 * h + 2, blk]
-        qy.own(ref, ref)
-
-    q_own(0)
-    q_sib(y)
+    def q_onward(j):
+        for i, (d, g) in enumerate(zip((PLUS, MINUS), qgot[j])):
+            g.wait()
+            ref = WQ.at[j, at("y", R - d) * 2 + c]
+            if i == j // 2:
+                send(qys, ref, ref, {"y": at("y", d)}, qfar[j])
+            send(qys, ref, ref, sib, qsib)
+
+    def q_last(j):
+        qfar[j].wait()
+        ref = WQ.at[j, at("y", FAR) * 2 + c]
+        send(qys, ref, ref, sib, qsib)
+
+    for j in (0, 2, 1):
+        q_own(j)
     z_onward(1)
     z_own(3)
     xr.wait()
     xr.onward()
     n_sib(at("x", MINUS), nsib[0])
     n_sib(at("x", PLUS), nsib[0])
+
+    og.wait()
+    OS[...] = PB[:, :, x] + OR[0] + OR[1] + OR[2]
+    zs2, zg2 = Sends(OD.at[0:R - 1]), Got(OD.at[0:R - 1])
+    os.wait()
+    sends.remove(os)
+
+    def o_send():
+        for dc in range(2):
+            c2 = oc if dc else c
+            for d in (PLUS, MINUS, FAR):
+                send(zs2, OS.at[at("z", d), c2], OD.at[z, :, span(c, B)], {"z": at("z", d), "c": c2}, zg2)
+        send(os2, OS.at[z, oc], OD.at[z, :, span(c, B)], sib, og2)
+        OD[z, :, span(c, B)] = OS[z, c]
+
+    os2, og2 = Sends(OD.at[0, :, 0:B]), Got(OD.at[0, :, 0:B])
 
     units = [[(0, 0, 3)], [(1, 0, 3)], [(0, 3, R), (1, 3, R)], [(2, 0, R)], [(3, 0, R)]]
     asend = Sends(AF.at[:, :, 0:NQ * 7 * B])
@@ -322,8 +365,11 @@
     act(2)
     a_onward(1)
     z_onward(3)
+    q_onward(0)
+    q_onward(2)
     for p in range(NP):
         w_own(p)
+    o_send()
     a_onward(2)
     zr[2].wait_far()
     act(3)
@@ -332,16 +378,16 @@
     a_onward(3)
     w_onward(0)
     a_onward(4)
-    q_own(1)
+    q_own(3)
+    q_onward(1)
     w_onward(1)
-    for d in l_ob:
-        d.wait()
     l_wd.wait()
-    l_wo.wait()
 
     zk = [z, at("z", MINUS), at("z", PLUS), at("z", FAR)]
-    rsend, nsend = Sends(RB), Got
-    rgot = [[Got(RB.at[k, :, 0:H]) for _ in range(2)] for k in range(R)]
+    rsend = [Sends(RB.at[0:R - 1]), Sends(RB.at[0])]
+    block = RB.at[0, 0, 0, 0:H]
+    rgot = [[Got(RB.at[k, :, :, 0:H]) if k == R - 1 else [Got(block), Got(block), Got(RB.at[k, 0:2, :, 0:H])]
+             for _ in range(2)] for k in range(R)]
     ngot = [Got(N2.at[:, 0:H]) for _ in range(2)]
     xgot, xsend = [Got(xo.at[0:7 * B]), Got(xo.at[0:24 * B])], Sends(xo.at[0:31 * B])
     nsend = new("s")
@@ -351,20 +397,36 @@
 
     def down(k, h):
         t = halves(h)
-        a, oo = AF[:, t, :].reshape(2 * B, D), OB[:, t, :].reshape(2 * B, DZ)
-        p = (jnp.dot(a, WD[zk[k], 0:D, :], preferred_element_type=F32)
-             + jnp.dot(oo, WD[zk[k], D:PK, :], preferred_element_type=F32))
-        PB[k, :, t, :] = p.reshape(R, H, 2 * B)
-        for i, d in enumerate(DIST):
-            if i:
-                send(rsend, PB.at[k, i, t], RB.at[k, i - 1, t], {"x": at("x", d)}, rgot[k][h])
+        p = jnp.dot(AF[:, t, :].reshape(2 * B, D), WD[zk[k]], preferred_element_type=F32)
+        for i in range(2):
+            PB[k, i, :, t] = p[:, i * B:(i + 1) * B].reshape(R, H, B)
+        if k == R - 1:
+            for i, d in enumerate(DIST):
+                if i:
+                    send(rsend[1], PB.at[k, :, i, t], RB.at[k, i - 1, :, t], {"x": at("x", d)}, rgot[k][h])
+            return
+        for i, d in enumerate((PLUS, MINUS)):
+            to = {"x": at("x", d)}
+            send(rsend[0], PB.at[k, i, R - 1, t], RB.at[k, R - 2, i, t], to, rgot[k][h][i])
+            send(rsend[0], PB.at[k, 1 - i, 1 + i, t], RB.at[k, i, 1 - i, t], to, rgot[k][h][2])
+
+    def add(k, h):
+        t = halves(h)
+        for i, d in enumerate((PLUS, MINUS)):
+            rgot[k][h][i].wait()
+            PB[k, i, 1 + i, t] = PB[k, i, 1 + i, t] + RB[k, R - 2, i, t]
+            send(rsend[0], PB.at[k, i, 1 + i, t], RB.at[k, i, i, t], {"x": at("x", d)}, rgot[k][h][2])
 
     def resid(k, h):
         t = halves(h)
-        rgot[k][h].wait()
-        yy = PB[k, 0, t] + RB[k, 0, t] + RB[k, 1, t] + RB[k, 2, t]
+        (rgot[k][h] if k == R - 1 else rgot[k][h][2]).wait()
         cols = span(y, 2 * B)
-        XP[k, t] = (XN[zk[k], t, cols].astype(F32) + yy).astype(BF)
+        for i in range(2):
+            part = slice(i * B, (i + 1) * B)
+            yy = OD[zk[k], t, part] + PB[k, i, 0, t] + RB[k, 0, i, t] + RB[k, 1, i, t]
+            if k == R - 1:
+                yy = yy + RB[k, 2, i, t]
+            XP[k, t, part] = (XN[zk[k], t, span(y * 2 + i, B)].astype(F32) + yy).astype(BF)
         dst = N2.at[zk[k], t, cols]
         for d in range(R):
             cp = pltpu.make_async_remote_copy(
@@ -409,36 +471,40 @@
     down(0, 1)
     w_onward(2)
     w_onward(3)
+    wsib[1].wait()
+    add(0, 0)
+    down(1, 0)
+    add(0, 1)
+    down(1, 1)
+    wsib[2].wait()
+    down(2, 0)
+    add(1, 0)
+    down(2, 1)
+    add(1, 1)
+    og2.wait()
+    zg2.wait()
     resid(0, 0)
-    w_onward(4)
-    wsib[1].wait()
-    down(1, 0)
-    down(1, 1)
     resid(0, 1)
     x_out(0)
-    qy.wait()
-    qy.onward()
-    q_sib(at("y", MINUS))
-    q_sib(at("y", PLUS))
-    wsib[2].wait()
-    down(2, 0)
-    down(2, 1)
-    far(2)
+    q_onward(3)
+    q_last(0)
+    q_last(2)
+    add(2, 0)
     resid(1, 0)
+    add(2, 1)
     resid(1, 1)
     x_out(1)
-    far(3)
+    far(2)
     resid(2, 0)
-    far(4)
+    far(len(wfar))
     resid(2, 1)
     x_out(2)
-    far(len(wfar))
     wsib[3].wait()
     down(3, 0)
     down(3, 1)
-    qy.wait_far()
-    q_sib(at("y", FAR))
     resid(3, 0)
+    q_last(1)
+    q_last(3)
     resid(3, 1)
     x_out(3)
     qsib.wait()
@@ -462,8 +528,9 @@
         for j in range(3):
             cols = slice(j * 3 * B, (j + 1) * 3 * B)
             w = WQ[:, :, :, cols].reshape(D, 3 * B)
-            QB[t, cols] = jnp.dot(N2B[t, :], w, preferred_element_type=F32).astype(BF)
-        qo[ahead(((z * 2 + c) * R + y) * B + h * H, H, H), :] = QB[t, :]
+            qo[ahead(((z * 2 + c) * R + y) * B + h * H, H, H), cols] = jnp.dot(
+                N2B[t, :], w, preferred_element_type=F32).astype(BF)
+            fan[h](cols)
 
     def out_sib(ref):
         send(osend, ref, ref, sib, osib)
@@ -473,7 +540,7 @@
     def coming(name, ref, then, whole):
         todo[name] = (Got(ref), then, whole)
 
-    def fan(h):
+    def arrivals(h):
         first, second = "yz" if h == 0 else "zy"
 
         def block(i, j, off, n):
@@ -501,7 +568,7 @@
 
         full = [(0, H, "")]
         go = {name: across(name, i, full) for name, i in (("o", 0), ("m", MINUS), ("p", PLUS))}
-        far = across("f", FAR, [(0, Q, "0"), (Q, Q, "1")])
+        across("f", FAR, [(0, Q, "0"), (Q, Q, "1")])
         for u, (d, name) in enumerate(((PLUS, "m"), (MINUS, "p"))):
             def onward(u=u, d=d, name=name):
                 hop(first, d, block(R - d, 0, u * Q, Q), f"r{h}{u}")
@@ -513,17 +580,22 @@
                 for d in (PLUS, MINUS):
                     hop(second, d, block(FAR, 0, u * Q, Q), f"s{h}f{u}{d}")
             coming(f"r{h}{u}", ref, rest, ref)
-        own = block(0, 0, 0, H)
-        for d in (PLUS, MINUS):
-            hop(first, d, own, f"f{h}{d}")
-        go["o"]()
-        out_sib(own)
-
+
+        def own(cols):
+            ref = block(0, 0, 0, H).at[:, cols]
+            for d in (PLUS, MINUS):
+                hop(first, d, ref, f"f{h}{d}")
+            for d in (PLUS, MINUS):
+                hop(second, d, ref, f"s{h}o{d}")
+            out_sib(ref)
+        return own
+
+    fan = [arrivals(h) for h in range(2)]
     for h in range(2):
         qkv(h)
-        fan(h)
     x_onward()
-    for key in "f0 s0o s1o f1 r0 s0m l1o s0p s1m l0o r1 s1p s0f0 l1m s0f1 s1f0 l0m s1f1 l0p l1p l0f l1f".split():
+    for key in ("f0", "s0o", "s1o", "f1", "r0", "s0m", "l1o", "s0p", "s1m", "l0o", "r1", "s1p",
+                "s0f0", "l1m", "s0f1", "s1f0", "l0m", "s1f1", "l0p", "l1p", "l0f", "l1f"):
         for name in [n for n in todo if n.startswith(key)]:
             got, then, ref = todo.pop(name)
             got.wait()
@@ -546,6 +618,18 @@
         pltpu.make_async_copy(N2, N2, ss.at[nsend]).wait()
 
 
+def _copy(a, b, c, d, sem):
+    n = 4
+    cps = []
+    for i, (src, dst) in enumerate(((a, c), (b, d))):
+        for j in range(n):
+            r = slice(j * D // n, (j + 1) * D // n)
+            cps.append(pltpu.make_async_copy(src.at[r], dst.at[r], sem.at[i, j]))
+            cps[-1].start()
+    for cp in cps:
+        cp.wait()
+
+
 def solution(mesh):
     mesh4 = Mesh(mesh.devices.reshape(R, R, R, 2), ("x", "z", "y", "c"))
 
@@ -553,7 +637,7 @@
         vm = pltpu.VMEM
         anyspec = pl.BlockSpec(memory_space=pl.ANY)
         sem = pltpu.SemaphoreType.DMA
-        return pl.pallas_call(
+        outs = pl.pallas_call(
             _kernel,
             out_shape=(vm((D, B), BF), vm((D, W), BF)),
             in_specs=[anyspec] * 9,
@@ -567,21 +651,33 @@
                 vm((NQ, D, 2 * B), BF),
                 vm((NQ, 2, R, B, B), BF),
                 vm((R, B, D), BF),
-                vm((R, B, DZ), BF),
-                vm((R, PK, 2 * B), BF),
-                vm((R, R, B, 2 * B), F32),
-                vm((R, R - 1, B, 2 * B), F32),
+                vm((R, 2 * B, DZ), BF),
+                vm((DZ, B), BF),
+                vm((R - 1, R, 2, B, B), F32),
+                vm((R, 2, B, B), F32),
+                vm((R, B, 2 * B), F32),
+                vm((R, D, 2 * B), BF),
+                vm((R, 2, R, B, B), F32),
+                vm((R, R - 1, 2, B, B), F32),
                 vm((R, B, 2 * B), BF),
                 vm((R, B, DZ), BF),
                 vm((B, D), BF),
                 vm((R, 8, B, W), BF),
-                vm((B, W), BF),
                 sem((NSEND,)), sem((NRECV,)), sem((NLOC,)),
             ],
             compiler_params=pltpu.CompilerParams(
-                collective_id=0, has_side_effects=True, vmem_limit_bytes=50 * 2**20),
+                collective_id=0, has_side_effects=True, vmem_limit_bytes=53 * 2**20),
             name="block",
         )(x.reshape(R, 2, R, B, B), g1.reshape(1, B), g2.reshape(1, B), w_gate, w_up, w_down, o, w_o, w_qkv)
+        return pl.pallas_call(
+            _copy,
+            out_shape=(jax.ShapeDtypeStruct((D, B), BF), jax.ShapeDtypeStruct((D, W), BF)),
+            in_specs=[pl.BlockSpec(memory_space=vm)] * 2,
+            out_specs=(anyspec, anyspec),
+            scratch_shapes=[sem((2, 4))],
+            compiler_params=pltpu.CompilerParams(vmem_limit_bytes=2**20),
+            name="store",
+        )(*outs)
 
     h = ("z", "y", "c")
     in_specs = (P(None, h), P(h), P(h), P(h, "x"), P(h, "x"), P("x", h), P(None, "x"), P("x", h), P(h, "x"))

time: 189 us -> 182 us (0.963)
  local copies, waits for them, and re-layouts: 4.71 us -> 0 us
  Pallas kernels: 184 us -> 181 us
    pallas_call x1, Pallas kernels: 184 us -> 177 us  [body(): pl.pallas_call(_kernel, out_shape=(vm((D, B), BF), vm((D, W), BF)), in_sp...]
    unnamed x2 -> x0, local copies, waits for them, and re-layouts: 4.71 us -> none
    pallas_call x0 -> x1, Pallas kernels: none -> 4.08 us  [body(): pl.pallas_call(_copy, out_shape=(jax.ShapeDtypeStruct((D, B), BF), jax.Sh...]
where the time goes in v3:
time: 182 us
  Pallas kernels  181 us (99%)
    pallas_call x1, Pallas kernels, body(): pl.pallas_call(_kernel, out_shape=(vm((D, B), BF), vm((D, W), BF)), in_sp...  177 us
    pallas_call x1, Pallas kernels, body(): pl.pallas_call(_copy, out_shape=(jax.ShapeDtypeStruct((D, B), BF), jax.Sh...  4.08 us

profile of v3, /device:TPU:1, one launch (start us, length us, event | category | flops | bytes accessed | tf_op | source)
XLA Modules:
  0.0 182.2 jit_solution(11560576961853927862)
XLA Ops:
  0.6 177.3 %block.1 = (bf16[4096,128]{1,0:T(8,128)(2,1)S(1)}, bf16[4096,1152]{1,0:T(8,128)(2,1)S(1)}) custom-call(bf16[4,2,4,128,128]{4,3,2,1,0:T(8,128)(2,1)} %bitcast.3, f32[1,128]{1,0:T(1,128)} %bitcast.4, f32[1,128]{1,0:T(1,128)} %bitcast.5, bf16[128,4096]{1,0:T(8,128)(2,1)} %wg.1, bf16[128,4096]{1,0:T(8,128)(2,1)} %wu.1, bf16[4096,128]{1,0:T(8,128)(2,1)} %wd.1, ...), custom_call_target="tpu_custom_call" | custom-call | tf_op jit(solution)/shard_map/block/pallas_call | solution.py:640
  177.9 4.1 %store.1 = (bf16[4096,128]{1,0:T(8,128)(2,1)}, bf16[4096,1152]{1,0:T(8,128)(2,1)}) custom-call(bf16[4096,128]{1,0:T(8,128)(2,1)S(1)} %get-tuple-element.4.a, bf16[4096,1152]{1,0:T(8,128)(2,1)S(1)} %get-tuple-element.5.b), custom_call_target="tpu_custom_call" | custom-call | tf_op jit(solution)/shard_map/store/pallas_call | solution.py:672

commit v4 on v3

--- a/solution.py
+++ b/solution.py
@@ -19,7 +19,7 @@
 NQ = 4
 NP = 4
 W = 1152
-NSEND, NRECV, NLOC = 30, 200, 20
+NSEND, NRECV, NLOC = 30, 216, 20
 
 
 def _kernel(x5, g1, g2, wg, wu, wd, o, wo, wq, xo, qo,
@@ -83,8 +83,8 @@
         return pl.ds(pl.multiple_of(b, step), n)
 
     bar = pltpu.get_barrier_semaphore()
-    peers = [(dx, dy, 0, 0) for dx in range(R) for dy in range(R) if dx + dy]
-    peers += [(0, dy, 0, 1) for dy in range(R)]
+    peers = [(dx, 0, 0, 0) for dx in range(1, R)]
+    peers += [(0, dy, 0, dc) for dy in range(R) for dc in range(2) if dy + dc]
     peers += [(0, 0, dz, dc) for dz in range(1, R) for dc in range(2)]
     for dx, dy, dz, dc in peers:
         pl.semaphore_signal(bar, inc=1, device_id={
@@ -161,29 +161,42 @@
     wds = Sends(WD.at[:, 0:D * 7 // 8, :])
     cuts = [(p, p * DZ, (p + 1) * DZ) for p in range(NP)]
     wgot = [[Got(WD.at[0, s:e, 0:B]), Got(WD.at[0, s:e, 0:B])] for _, s, e in cuts]
-    wsib = [Got(WD.at[0, :, 0:B]) for _ in range(3)] + [Got(WD.at[0, :, 0:B])]
-    wfar = []
-
-    def w_own(p):
-        _, s, e = cuts[p]
-        src, dst = wd.at[s:e, :], WD.at[z, s:e, span(c, B)]
-        for d, g in zip((PLUS, MINUS), wgot[p]):
-            send(wds, src, dst, {"z": at("z", d)}, g)
-        send(wds, src, dst, sib, wsib[0])
-
-    def w_onward(p):
-        _, s, e = cuts[p]
-        for h, (d, g) in enumerate(zip((PLUS, MINUS), wgot[p])):
+    piece = WD.at[0, 0:DZ, 0:B]
+    wsib, wnear = Got(WD.at[0, :, 0:B]), [[Got(piece), Got(piece)] for _ in range(NP)]
+    wfar, wlast = [[Got(piece), Got(piece)] for _ in range(2)], [Got(WD.at[0, 0:2 * DZ, 0:B]) for _ in range(2)]
+
+    def cut(i, h):
+        p = (i + 2 * h) % NP
+        return cuts[p]
+
+    def w_own(i):
+        for h, (d, g) in enumerate(zip((PLUS, MINUS), wgot[i])):
+            _, s, e = cut(i, h)
+            send(wds, wd.at[s:e, :], WD.at[z, s:e, span(c, B)], {"z": at("z", d)}, g)
+        _, s, e = cuts[i]
+        send(wds, wd.at[s:e, :], WD.at[z, s:e, span(c, B)], sib, wsib)
+
+    def w_onward(i):
+        for h, (d, g) in enumerate(zip((PLUS, MINUS), wgot[i])):
             g.wait()
-            lo, hi = max(s, h * D // 2), min(e, (h + 1) * D // 2)
-            zz = at("z", R - d)
-            if lo < hi:
-                ref = WD.at[zz, lo:hi, span(c, B)]
-                got = Got(ref)
-                send(wds, ref, ref, {"z": at("z", d)}, got)
-                wfar.append((got, lo, hi))
-            ref = WD.at[zz, s:e, span(c, B)]
-            send(wds, ref, ref, sib, wsib[1 + h])
+            _, s, e = cut(i, h)
+            ref = WD.at[at("z", R - d), s:e, span(c, B)]
+            send(wds, ref, ref, sib, wnear[i][h])
+
+    def w_near(h, ps):
+        for p in ps:
+            wnear[p][h].wait()
+
+    def w_far(h, lane):
+        d = (PLUS, MINUS)[h]
+        ref = WD.at[at("z", R - d), span(2 * h + c, DZ), lane * B:(lane + 1) * B]
+        send(wds, ref, ref, {"z": at("z", d)}, wfar[lane][h])
+
+    def far(lane):
+        for h, g in enumerate(wfar[lane]):
+            g.wait()
+            ref = WD.at[at("z", FAR), span(2 * h + c, DZ), lane * B:(lane + 1) * B]
+            send(wds, ref, ref, sib, wlast[lane])
 
     l_wo.wait()
     os, og = Sends(OR), Got(OR)
@@ -296,21 +309,17 @@
 
     og.wait()
     OS[...] = PB[:, :, x] + OR[0] + OR[1] + OR[2]
-    zs2, zg2 = Sends(OD.at[0:R - 1]), Got(OD.at[0:R - 1])
+    zs2, zg2 = Sends(OD.at[0:R - 1]), [Got(OD.at[0:2]), Got(OD.at[0])]
+    os2, og2 = Sends(OD.at[0, :, 0:B]), Got(OD.at[0, :, 0:B])
     os.wait()
     sends.remove(os)
 
-    def o_send():
-        for dc in range(2):
-            c2 = oc if dc else c
-            for d in (PLUS, MINUS, FAR):
-                send(zs2, OS.at[at("z", d), c2], OD.at[z, :, span(c, B)], {"z": at("z", d), "c": c2}, zg2)
-        send(os2, OS.at[z, oc], OD.at[z, :, span(c, B)], sib, og2)
-        OD[z, :, span(c, B)] = OS[z, c]
-
-    os2, og2 = Sends(OD.at[0, :, 0:B]), Got(OD.at[0, :, 0:B])
-
-    units = [[(0, 0, 3)], [(1, 0, 3)], [(0, 3, R), (1, 3, R)], [(2, 0, R)], [(3, 0, R)]]
+    def o_send(ds, got):
+        for d in ds:
+            for c2 in (c, oc):
+                send(zs2, OS.at[at("z", d), c2], OD.at[z, :, span(c, B)], {"z": at("z", d), "c": c2}, got)
+
+    units = [[(0, 0, 3)], [(1, 0, 3)], [(0, 3, R), (1, 3, R)], [(2, 0, 2)], [(2, 2, R)], [(3, 0, 2)], [(3, 2, R)]]
     asend = Sends(AF.at[:, :, 0:NQ * 7 * B])
     arest = Got(AF.at[:, :, 0:NQ * 3 * B])
     agot = []
@@ -369,15 +378,21 @@
     q_onward(2)
     for p in range(NP):
         w_own(p)
-    o_send()
+    o_send((PLUS, MINUS), zg2[0])
+    send(os2, OS.at[z, oc], OD.at[z, :, span(c, B)], sib, og2)
+    OD[z, :, span(c, B)] = OS[z, c]
     a_onward(2)
     zr[2].wait_far()
     act(3)
+    act(4)
     zr[3].wait_far()
-    act(4)
+    act(5)
+    act(6)
     a_onward(3)
+    a_onward(4)
     w_onward(0)
-    a_onward(4)
+    a_onward(5)
+    a_onward(6)
     q_own(3)
     q_onward(1)
     w_onward(1)
@@ -386,8 +401,8 @@
     zk = [z, at("z", MINUS), at("z", PLUS), at("z", FAR)]
     rsend = [Sends(RB.at[0:R - 1]), Sends(RB.at[0])]
     block = RB.at[0, 0, 0, 0:H]
-    rgot = [[Got(RB.at[k, :, :, 0:H]) if k == R - 1 else [Got(block), Got(block), Got(RB.at[k, 0:2, :, 0:H])]
-             for _ in range(2)] for k in range(R)]
+    rgot = [[[Got(block), Got(block), Got(RB.at[k, 0:2, :, 0:H])] for _ in range(2)] for k in range(R - 1)]
+    rlast = [[Got(RB.at[0, :, 0, 0:H]) for _ in range(2)] for _ in range(2)]
     ngot = [Got(N2.at[:, 0:H]) for _ in range(2)]
     xgot, xsend = [Got(xo.at[0:7 * B]), Got(xo.at[0:24 * B])], Sends(xo.at[0:31 * B])
     nsend = new("s")
@@ -395,16 +410,30 @@
     def halves(h):
         return slice(h * H, h * H + H)
 
+    def product(k, h, w, kk=slice(0, D)):
+        return jnp.dot(AF[:, halves(h), kk].reshape(2 * B, w.shape[0]), w, preferred_element_type=F32)
+
+    def early(k, h):
+        spans = [slice(0, D - DZ)] if k == 1 else [slice(2 * DZ, D), slice(0, DZ)]
+        p = sum(product(k, h, WD[zk[k], kk], kk) for kk in spans)
+        for i in range(2):
+            PB[k, i, :, halves(h)] = p[:, i * B:(i + 1) * B].reshape(R, H, B)
+
+    def down_last(i, h):
+        t, k = halves(h), R - 1
+        p = product(k, h, WD[zk[k], :, i * B:(i + 1) * B])
+        PB[k, i, :, t] = p.reshape(R, H, B)
+        for j, d in enumerate(DIST):
+            if j:
+                send(rsend[1], PB.at[k, i, j, t], RB.at[k, j - 1, i, t], {"x": at("x", d)}, rlast[i][h])
+
     def down(k, h):
         t = halves(h)
-        p = jnp.dot(AF[:, t, :].reshape(2 * B, D), WD[zk[k]], preferred_element_type=F32)
+        kk = (slice(0, D), slice(D - DZ, D), slice(DZ, 2 * DZ))[k]
+        p = product(k, h, WD[zk[k], kk], kk)
         for i in range(2):
-            PB[k, i, :, t] = p[:, i * B:(i + 1) * B].reshape(R, H, B)
-        if k == R - 1:
-            for i, d in enumerate(DIST):
-                if i:
-                    send(rsend[1], PB.at[k, :, i, t], RB.at[k, i - 1, :, t], {"x": at("x", d)}, rgot[k][h])
-            return
+            v = p[:, i * B:(i + 1) * B].reshape(R, H, B)
+            PB[k, i, :, t] = PB[k, i, :, t] + v if k else v
         for i, d in enumerate((PLUS, MINUS)):
             to = {"x": at("x", d)}
             send(rsend[0], PB.at[k, i, R - 1, t], RB.at[k, R - 2, i, t], to, rgot[k][h][i])
@@ -417,20 +446,30 @@
             PB[k, i, 1 + i, t] = PB[k, i, 1 + i, t] + RB[k, R - 2, i, t]
             send(rsend[0], PB.at[k, i, 1 + i, t], RB.at[k, i, i, t], {"x": at("x", d)}, rgot[k][h][2])
 
+    def finish(k, h, i, yy):
+        t, part = halves(h), slice(i * B, (i + 1) * B)
+        XP[k, t, part] = (XN[zk[k], t, span(y * 2 + i, B)].astype(F32) + (OD[zk[k], t, part] + PB[k, i, 0, t] + yy)).astype(BF)
+
     def resid(k, h):
         t = halves(h)
-        (rgot[k][h] if k == R - 1 else rgot[k][h][2]).wait()
-        cols = span(y, 2 * B)
+        rgot[k][h][2].wait()
         for i in range(2):
-            part = slice(i * B, (i + 1) * B)
-            yy = OD[zk[k], t, part] + PB[k, i, 0, t] + RB[k, 0, i, t] + RB[k, 1, i, t]
-            if k == R - 1:
-                yy = yy + RB[k, 2, i, t]
-            XP[k, t, part] = (XN[zk[k], t, span(y * 2 + i, B)].astype(F32) + yy).astype(BF)
-        dst = N2.at[zk[k], t, cols]
+            finish(k, h, i, RB[k, 0, i, t] + RB[k, 1, i, t])
+
+    def resid_last(i, h):
+        t, k = halves(h), R - 1
+        rlast[i][h].wait()
+        finish(k, h, i, RB[k, 0, i, t] + RB[k, 1, i, t] + RB[k, 2, i, t])
+
+    def tell(k, h, i=None):
+        t = halves(h)
+        if i is None:
+            src, dst = XP.at[k, t], N2.at[zk[k], t, span(y, 2 * B)]
+        else:
+            src, dst = XP.at[k, t, i * B:(i + 1) * B], N2.at[zk[k], t, span(y * 2 + i, B)]
         for d in range(R):
             cp = pltpu.make_async_remote_copy(
-                src_ref=XP.at[k, t], dst_ref=dst, send_sem=ss.at[nsend], recv_sem=rs.at[ngot[h].i],
+                src_ref=src, dst_ref=dst, send_sem=ss.at[nsend], recv_sem=rs.at[ngot[h].i],
                 device_id={"x": at("x", d), "y": x}, device_id_type=MESH)
             if d:
                 cp.start()
@@ -439,7 +478,7 @@
 
                 @pl.when(x == y)
                 def _():
-                    dst[...] = XP[k, t]
+                    dst[...] = src[...]
 
     def x_out(k):
         rows = xo.at[span((z * 2 + c) * R + x, B), :]
@@ -455,35 +494,37 @@
         for d in (PLUS, MINUS, FAR):
             send(xsend, ref, ref, {"x": at("x", d)}, xgot[1])
 
-    wdone = [0]
-
-    def far(n):
-        order = [wfar[i] for t in range(len(wfar) // 2) for i in (t, t + len(wfar) // 2)]
-        for g, s, e in order[wdone[0]:n]:
-            g.wait()
-            ref = WD.at[zk[3], s:e, span(c, B)]
-            send(wds, ref, ref, sib, wsib[3])
-        wdone[0] = n
-
     a_wait()
-    wsib[0].wait()
+    wsib.wait()
     down(0, 0)
     down(0, 1)
+    w_near(0, range(2))
+    w_near(1, range(2))
+    for lane in range(2):
+        w_far(0, lane)
+        w_far(1, lane)
+    o_send((FAR,), zg2[1])
     w_onward(2)
+    w_near(0, (2,))
+    early(1, 0)
     w_onward(3)
-    wsib[1].wait()
+    early(1, 1)
     add(0, 0)
+    w_near(0, (NP - 1,))
     down(1, 0)
+    w_near(1, (2, NP - 1))
+    down(1, 1)
     add(0, 1)
-    down(1, 1)
-    wsib[2].wait()
+    early(2, 0)
     down(2, 0)
+    early(2, 1)
+    down(2, 1)
     add(1, 0)
-    down(2, 1)
     add(1, 1)
     og2.wait()
-    zg2.wait()
+    zg2[0].wait()
     resid(0, 0)
+    tell(0, 0)
     resid(0, 1)
     x_out(0)
     q_onward(3)
@@ -491,21 +532,36 @@
     q_last(2)
     add(2, 0)
     resid(1, 0)
+    tell(1, 0)
     add(2, 1)
+    far(0)
     resid(1, 1)
     x_out(1)
-    far(2)
+    wlast[0].wait()
+    down_last(0, 0)
+    down_last(0, 1)
     resid(2, 0)
-    far(len(wfar))
+    tell(2, 0)
+    far(1)
+    tell(0, 1)
+    wlast[1].wait()
+    down_last(1, 0)
+    down_last(1, 1)
     resid(2, 1)
     x_out(2)
-    wsib[3].wait()
-    down(3, 0)
-    down(3, 1)
-    resid(3, 0)
+    zg2[1].wait()
+    resid_last(0, 0)
+    tell(3, 0, 0)
+    resid_last(0, 1)
     q_last(1)
     q_last(3)
-    resid(3, 1)
+    resid_last(1, 0)
+    tell(3, 0, 1)
+    tell(1, 1)
+    tell(2, 1)
+    tell(3, 1, 0)
+    resid_last(1, 1)
+    tell(3, 1, 1)
     x_out(3)
     qsib.wait()
 

time: 182 us -> 182 us (level)
  no operation moved by 1% of the time
where the time goes in v4:
time: 182 us; the launch traced here: 181 us
  Pallas kernels  181 us (99%)
    pallas_call x1, Pallas kernels, body(): pl.pallas_call(_kernel, out_shape=(vm((D, B), BF), vm((D, W), BF)), in_sp...  177 us
    pallas_call x1, Pallas kernels, body(): pl.pallas_call(_copy, out_shape=(jax.ShapeDtypeStruct((D, B), BF), jax.Sh...  4.08 us

profile of v4, /device:TPU:1, one launch (start us, length us, event | category | flops | bytes accessed | tf_op | source)
XLA Modules:
  0.0 181.4 jit_solution(15447335410935212210)
XLA Ops:
  0.6 176.5 %block.1 = (bf16[4096,128]{1,0:T(8,128)(2,1)S(1)}, bf16[4096,1152]{1,0:T(8,128)(2,1)S(1)}) custom-call(bf16[4,2,4,128,128]{4,3,2,1,0:T(8,128)(2,1)} %bitcast.3, f32[1,128]{1,0:T(1,128)} %bitcast.4, f32[1,128]{1,0:T(1,128)} %bitcast.5, bf16[128,4096]{1,0:T(8,128)(2,1)} %wg.1, bf16[128,4096]{1,0:T(8,128)(2,1)} %wu.1, bf16[4096,128]{1,0:T(8,128)(2,1)} %wd.1, ...), custom_call_target="tpu_custom_call" | custom-call | tf_op jit(solution)/shard_map/block/pallas_call | solution.py:696
  177.2 4.1 %store.1 = (bf16[4096,128]{1,0:T(8,128)(2,1)}, bf16[4096,1152]{1,0:T(8,128)(2,1)}) custom-call(bf16[4096,128]{1,0:T(8,128)(2,1)S(1)} %get-tuple-element.4.a, bf16[4096,1152]{1,0:T(8,128)(2,1)S(1)} %get-tuple-element.5.b), custom_call_target="tpu_custom_call" | custom-call | tf_op jit(solution)/shard_map/store/pallas_call | solution.py:728

commit v5 on v4

--- a/solution.py
+++ b/solution.py
@@ -19,7 +19,7 @@
 NQ = 4
 NP = 4
 W = 1152
-NSEND, NRECV, NLOC = 30, 216, 20
+NSEND, NRECV, NLOC = 21, 156, 19
 
 
 def _kernel(x5, g1, g2, wg, wu, wd, o, wo, wq, xo, qo,
@@ -134,7 +134,7 @@
         def __init__(self, axis, sends, own, half):
             self.axis, self.sends, self.half = axis, sends, half
             self.got = [Got(own), Got(own)]
-            self.far = [Got(half(0, 0)), Got(half(0, 1))]
+            self.far = Got(own)
 
         def own(self, src, dst):
             for d, g in zip((PLUS, MINUS), self.got):
@@ -145,13 +145,12 @@
                 g.wait()
 
         def onward(self):
-            for h, (d, g) in enumerate(zip((PLUS, MINUS), self.far)):
+            for h, d in enumerate((PLUS, MINUS)):
                 ref = self.half(at(self.axis, R - d), h)
-                send(self.sends, ref, ref, {self.axis: at(self.axis, d)}, g)
+                send(self.sends, ref, ref, {self.axis: at(self.axis, d)}, self.far)
 
         def wait_far(self):
-            for g in self.far:
-                g.wait()
+            self.far.wait()
 
     send_a2a(0)
     send_a2a(1)
@@ -321,11 +320,11 @@
 
     units = [[(0, 0, 3)], [(1, 0, 3)], [(0, 3, R), (1, 3, R)], [(2, 0, 2)], [(2, 2, R)], [(3, 0, 2)], [(3, 2, R)]]
     asend = Sends(AF.at[:, :, 0:NQ * 7 * B])
-    arest = Got(AF.at[:, :, 0:NQ * 3 * B])
+    arest = Got(AF.at[:, :, 0:NQ * 5 * B])
     agot = []
     for u in units:
         n = AF.at[0:sum(hi - lo for _, lo, hi in u), :, 0:B]
-        agot.append([[Got(n), Got(n)] for _ in range(2)])
+        agot.append([Got(n), Got(n)])
     NF4 = NF.reshape(2, R, B, D)
 
     def act(u):
@@ -344,22 +343,16 @@
                     for c1 in range(2):
                         @pl.when(c == c1)
                         def _():
-                            send(asend, AL.at[q, c2, lo:hi], dst, {"y": at("y", d), "c": c2}, agot[u][i][c1])
+                            send(asend, AL.at[q, c2, lo:hi], dst, {"y": at("y", d), "c": c2}, agot[u][i] if c1 == i else arest)
             send(asend, AL.at[q, oc, lo:hi], dst, sib, arest)
             AF[lo:hi, :, col] = AL[q, c, lo:hi]
 
     def a_onward(u):
         for i, d in enumerate((PLUS, MINUS)):
-            agot[u][i][i].wait()
+            agot[u][i].wait()
             for q, lo, hi in units[u]:
                 ref = AF.at[lo:hi, :, span((at("y", R - d) * 2 + i) * NQ + q, B)]
                 send(asend, ref, ref, {"y": at("y", d)}, arest)
-
-    def a_wait():
-        for u in range(len(units)):
-            for i in range(2):
-                agot[u][i][1 - i].wait()
-        arest.wait()
 
     nsib[0].wait()
     zr[0].wait_far()
@@ -378,7 +371,6 @@
     q_onward(2)
     for p in range(NP):
         w_own(p)
-    o_send((PLUS, MINUS), zg2[0])
     send(os2, OS.at[z, oc], OD.at[z, :, span(c, B)], sib, og2)
     OD[z, :, span(c, B)] = OS[z, c]
     a_onward(2)
@@ -494,7 +486,7 @@
         for d in (PLUS, MINUS, FAR):
             send(xsend, ref, ref, {"x": at("x", d)}, xgot[1])
 
-    a_wait()
+    arest.wait()
     wsib.wait()
     down(0, 0)
     down(0, 1)
@@ -503,6 +495,7 @@
     for lane in range(2):
         w_far(0, lane)
         w_far(1, lane)
+    o_send((PLUS, MINUS), zg2[0])
     o_send((FAR,), zg2[1])
     w_onward(2)
     w_near(0, (2,))
@@ -522,7 +515,6 @@
     add(1, 0)
     add(1, 1)
     og2.wait()
-    zg2[0].wait()
     resid(0, 0)
     tell(0, 0)
     resid(0, 1)
@@ -531,24 +523,23 @@
     q_last(0)
     q_last(2)
     add(2, 0)
-    resid(1, 0)
-    tell(1, 0)
     add(2, 1)
     far(0)
-    resid(1, 1)
-    x_out(1)
     wlast[0].wait()
     down_last(0, 0)
     down_last(0, 1)
-    resid(2, 0)
-    tell(2, 0)
+    tell(0, 1)
     far(1)
-    tell(0, 1)
     wlast[1].wait()
     down_last(1, 0)
     down_last(1, 1)
-    resid(2, 1)
-    x_out(2)
+    zg2[0].wait()
+    for k in (1, 2):
+        resid(k, 0)
+        tell(k, 0)
+    for k in (1, 2):
+        resid(k, 1)
+        x_out(k)
     zg2[1].wait()
     resid_last(0, 0)
     tell(3, 0, 0)

time: 182 us -> 180 us (0.989)
  Pallas kernels: 181 us -> 179 us
where the time goes in v5:
time: 180 us
  Pallas kernels  179 us (99%)
    pallas_call x1, Pallas kernels, body(): pl.pallas_call(_kernel, out_shape=(vm((D, B), BF), vm((D, W), BF)), in_sp...  175 us
    pallas_call x1, Pallas kernels, body(): pl.pallas_call(_copy, out_shape=(jax.ShapeDtypeStruct((D, B), BF), jax.Sh...  4.08 us

profile of v5, /device:TPU:1, one launch (start us, length us, event | category | flops | bytes accessed | tf_op | source)
XLA Modules:
  0.0 179.7 jit_solution(4815886324947005083)
XLA Ops:
  0.6 174.8 %block.1 = (bf16[4096,128]{1,0:T(8,128)(2,1)S(1)}, bf16[4096,1152]{1,0:T(8,128)(2,1)S(1)}) custom-call(bf16[4,2,4,128,128]{4,3,2,1,0:T(8,128)(2,1)} %bitcast.3, f32[1,128]{1,0:T(1,128)} %bitcast.4, f32[1,128]{1,0:T(1,128)} %bitcast.5, bf16[128,4096]{1,0:T(8,128)(2,1)} %wg.1, bf16[128,4096]{1,0:T(8,128)(2,1)} %wu.1, bf16[4096,128]{1,0:T(8,128)(2,1)} %wd.1, ...), custom_call_target="tpu_custom_call" | custom-call | tf_op jit(solution)/shard_map/block/pallas_call | solution.py:687
  175.5 4.1 %store.1 = (bf16[4096,128]{1,0:T(8,128)(2,1)}, bf16[4096,1152]{1,0:T(8,128)(2,1)}) custom-call(bf16[4096,128]{1,0:T(8,128)(2,1)S(1)} %get-tuple-element.4.a, bf16[4096,1152]{1,0:T(8,128)(2,1)S(1)} %get-tuple-element.5.b), custom_call_target="tpu_custom_call" | custom-call | tf_op jit(solution)/shard_map/store/pallas_call | solution.py:719

commit v6 on v5

--- a/solution.py
+++ b/solution.py
@@ -524,11 +524,11 @@
     q_last(2)
     add(2, 0)
     add(2, 1)
+    tell(0, 1)
     far(0)
     wlast[0].wait()
     down_last(0, 0)
     down_last(0, 1)
-    tell(0, 1)
     far(1)
     wlast[1].wait()
     down_last(1, 0)

time: 180 us -> 180 us (level)
  no operation moved by 1% of the time
where the time goes in v6:
time: 180 us
  Pallas kernels  179 us (99%)
    pallas_call x1, Pallas kernels, body(): pl.pallas_call(_kernel, out_shape=(vm((D, B), BF), vm((D, W), BF)), in_sp...  175 us
    pallas_call x1, Pallas kernels, body(): pl.pallas_call(_copy, out_shape=(jax.ShapeDtypeStruct((D, B), BF), jax.Sh...  4.08 us

profile of v6, /device:TPU:1, one launch (start us, length us, event | category | flops | bytes accessed | tf_op | source)
XLA Modules:
  0.0 179.6 jit_solution(11498788928771225636)
XLA Ops:
  0.6 174.7 %block.1 = (bf16[4096,128]{1,0:T(8,128)(2,1)S(1)}, bf16[4096,1152]{1,0:T(8,128)(2,1)S(1)}) custom-call(bf16[4,2,4,128,128]{4,3,2,1,0:T(8,128)(2,1)} %bitcast.3, f32[1,128]{1,0:T(1,128)} %bitcast.4, f32[1,128]{1,0:T(1,128)} %bitcast.5, bf16[128,4096]{1,0:T(8,128)(2,1)} %wg.1, bf16[128,4096]{1,0:T(8,128)(2,1)} %wu.1, bf16[4096,128]{1,0:T(8,128)(2,1)} %wd.1, ...), custom_call_target="tpu_custom_call" | custom-call | tf_op jit(solution)/shard_map/block/pallas_call | solution.py:687
  175.3 4.1 %store.1 = (bf16[4096,128]{1,0:T(8,128)(2,1)}, bf16[4096,1152]{1,0:T(8,128)(2,1)}) custom-call(bf16[4096,128]{1,0:T(8,128)(2,1)S(1)} %get-tuple-element.4.a, bf16[4096,1152]{1,0:T(8,128)(2,1)S(1)} %get-tuple-element.5.b), custom_call_target="tpu_custom_call" | custom-call | tf_op jit(solution)/shard_map/store/pallas_call | solution.py:719

commit v7 on v6

--- a/solution.py
+++ b/solution.py
@@ -537,12 +537,12 @@
     for k in (1, 2):
         resid(k, 0)
         tell(k, 0)
+    zg2[1].wait()
+    resid_last(0, 0)
+    tell(3, 0, 0)
     for k in (1, 2):
         resid(k, 1)
         x_out(k)
-    zg2[1].wait()
-    resid_last(0, 0)
-    tell(3, 0, 0)
     resid_last(0, 1)
     q_last(1)
     q_last(3)

time: 180 us -> 180 us (level)
  no operation moved by 1% of the time
where the time goes in v7:
time: 180 us
  Pallas kernels  179 us (99%)
    pallas_call x1, Pallas kernels, body(): pl.pallas_call(_kernel, out_shape=(vm((D, B), BF), vm((D, W), BF)), in_sp...  175 us
    pallas_call x1, Pallas kernels, body(): pl.pallas_call(_copy, out_shape=(jax.ShapeDtypeStruct((D, B), BF), jax.Sh...  4.08 us

profile of v7, /device:TPU:1, one launch (start us, length us, event | category | flops | bytes accessed | tf_op | source)
XLA Modules:
  0.0 179.6 jit_solution(279985412750759291)
XLA Ops:
  0.6 174.7 %block.1 = (bf16[4096,128]{1,0:T(8,128)(2,1)S(1)}, bf16[4096,1152]{1,0:T(8,128)(2,1)S(1)}) custom-call(bf16[4,2,4,128,128]{4,3,2,1,0:T(8,128)(2,1)} %bitcast.3, f32[1,128]{1,0:T(1,128)} %bitcast.4, f32[1,128]{1,0:T(1,128)} %bitcast.5, bf16[128,4096]{1,0:T(8,128)(2,1)} %wg.1, bf16[128,4096]{1,0:T(8,128)(2,1)} %wu.1, bf16[4096,128]{1,0:T(8,128)(2,1)} %wd.1, ...), custom_call_target="tpu_custom_call" | custom-call | tf_op jit(solution)/shard_map/block/pallas_call | solution.py:687
  175.3 4.1 %store.1 = (bf16[4096,128]{1,0:T(8,128)(2,1)}, bf16[4096,1152]{1,0:T(8,128)(2,1)}) custom-call(bf16[4096,128]{1,0:T(8,128)(2,1)S(1)} %get-tuple-element.4.a, bf16[4096,1152]{1,0:T(8,128)(2,1)S(1)} %get-tuple-element.5.b), custom_call_target="tpu_custom_call" | custom-call | tf_op jit(solution)/shard_map/store/pallas_call | solution.py:719
